TPU v7x, 128 devices: a whole 4x4x4 slice. The times are simulated.
128 devices in a mesh: rows: 32 (over y, z, core), tgt: 4 (over x).
Axes of the slice: x: 4, y: 4, z: 4, core: 2. Of those that a mesh axis runs over, the one named last changes fastest.
Arguments:
- frames: bfloat16 [65536, 512], P('rows', 'tgt'), may hold values from -6 to 6
- weights: bfloat16 [512, 1024], replicated, may hold values from -0.25 to 0.25
- phases: float32 [1024], replicated, may hold values from -3.140625 to 3.140625
- residual: float32 [65536, 1024], P('rows', 'tgt'), may hold values from -6 to 6
Outputs:
- residual_next: float32 [65536, 1024], P('rows', 'tgt')
- coefficients: float32 [1024, 1024], P(None, 'tgt')
All inputs are finite; a program needn't handle non-finite values.
Results may differ from a plain program's by a relative error of at most 0.0003.
Values may be sent and summed in bfloat16 or wider, within the bound.
No kernel may reach another device: no remote copies, remote signals or barrier semaphores. Data moves between devices by JAX's collectives and lax.ppermute only.
A program may use at most 128 MiB of HBM per device.

v0:
```python
import jax
import jax.numpy as jnp
from jax import lax
from jax.sharding import PartitionSpec as P


def laid_out(parts, dim):
    parts = jnp.moveaxis(parts, 0, dim)
    shape = parts.shape
    return parts.reshape(*shape[:dim], shape[dim] * shape[dim + 1], *shape[dim + 2 :])


def from_everyone(value, axis):
    count = lax.axis_size(axis)
    return lax.all_to_all(
        jnp.broadcast_to(value[None], (count, *value.shape)), axis, 0, 0, tiled=True
    )


def gathered_copies(value, axis, dim):
    return laid_out(from_everyone(value, axis), dim)


def cut_along(value, dim, count):
    before, after = (value.shape[:dim], value.shape[dim + 1 :])
    return jnp.moveaxis(value.reshape(*before, count, -1, *after), dim, 0)


def sent_and_summed(value, axis, dim):
    count = lax.axis_size(axis)
    parts = lax.all_to_all(cut_along(value, dim, count), axis, 0, 0, tiled=True)
    return jnp.sum(parts, axis=0)


def gram_of(row_block):
    return jnp.dot(
        row_block.T, row_block, precision=lax.Precision.HIGHEST, preferred_element_type=jnp.float32
    )


def body(frames, weights, phases, residual):
    highest = lax.Precision.HIGHEST
    rows_here = frames.shape[0]
    feature_count = weights.shape[1]
    preact = jnp.dot(gathered_copies(frames, "tgt", 1), weights, preferred_element_type=jnp.float32)
    feature = jnp.sqrt(2.0 / feature_count) * jnp.cos(preact + phases[None, :])
    gram_matrix = lax.psum(gram_of(feature), "rows")
    total_rows = rows_here * lax.axis_size("rows")
    gram_matrix = gram_matrix + 0.1 * total_rows / feature_count * jnp.eye(
        feature_count, dtype=jnp.float32
    )
    factor = jnp.linalg.cholesky(gram_matrix)
    correlation = jnp.dot(
        feature.T, residual, precision=highest, preferred_element_type=jnp.float32
    )
    own_corr = sent_and_summed(correlation, "rows", 1)
    own_coef = jax.scipy.linalg.cho_solve((factor, True), own_corr)
    coefficients = gathered_copies(own_coef, "rows", 1)
    residual_next = residual - jnp.dot(
        feature, coefficients, precision=highest, preferred_element_type=jnp.float32
    )
    return (residual_next, coefficients)


def solution(mesh):
    return jax.shard_map(
        body,
        mesh=mesh,
        in_specs=(P("rows", "tgt"), P(), P(), P("rows", "tgt")),
        out_specs=(P("rows", "tgt"), P(None, "tgt")),
        check_vma=False,
    )
```

profile of v0, /device:TPU:1, one launch (start us, length us, event | category | flops | bytes accessed | tf_op | source)
XLA Modules:
  0.0 641.0 jit_solution(1232279628602175315)
XLA Ops:
  7.2 1.3 copy.45
  8.8 30.1 %all_to_all.15 = bf16[4,2048,128]{1,2,0:T(8,128)(2,1)S(1)} all-to-all(bf16[4,2048,128]{1,2,0:T(8,128)(2,1)S(1)} %broadcast_in_dim.5), channel_id=1, replica_groups=mesh['rows'=32,'tgt'=4] {'tgt'}, dimensions={0} | all-to-all | bytes 4194304 | tf_op jit(solution)/shard_map/all_to_all | solution.py:15
  38.9 2.4 fusion.110
  41.4 3.2 copy-done.2
  44.6 26.9 %cosine_multiply_fusion.12 = f32[2048,1024]{1,0:T(8,128)S(1)} fusion(f32[2048,1024]{1,0:T(8,128)S(1)} %fusion.110, f32[1024]{0:T(1024)S(1)} %copy-done.5), kind=kLoop, calls=%fused_computation.2.clone.2.clone.2 | loop fusion | flops 4194304 | bytes 16781312 | tf_op jit(solution)/shard_map/dot_general | solution.py:36
  71.5 29.3 %fusion.2 = f32[1024,1024]{0,1:T(8,128)} fusion(f32[2048,1024]{1,0:T(8,128)S(1)} %cosine_multiply_fusion.12), kind=kOutput, calls=%fused_computation.5 | convolution fusion | flops 25769803776 | bytes 12582912 | tf_op jit(solution)/shard_map/dot_general | solution.py:36
  100.9 1.6 copy-done.4
  102.4 42.3 %fusion.11 = f32[32,1024,8]{1,2,0:T(8,128)} fusion(f32[2048,256]{1,0:T(8,128)S(1)} %copy-done.4, f32[2048,1024]{1,0:T(8,128)} %copy-done.2, f32[1024]{0:T(1024)S(1)} %copy-done.5), kind=kOutput, calls=%fused_computation.19 | convolution fusion | flops 6446645248 | bytes 11538432 | tf_op jit(solution)/shard_map/dot_general | solution.py:53
  144.8 9.9 %all-to-all-start.1 = ((f32[32,1024,8]{1,2,0:T(8,128)}), f32[32,1024,8]{1,2,0:T(8,128)S(1)}, u32[]{:S(2)}, u32[]{:S(2)}) async-start(f32[32,1024,8]{1,2,0:T(8,128)} %fusion.11), calls=%async_computation.1 | async-start | bytes 2097152 | tf_op jit(solution)/shard_map/all_to_all | solution.py:31
  154.7 16.9 %all-to-all-done.1 = f32[32,1024,8]{1,2,0:T(8,128)S(1)} async-done(((f32[32,1024,8]{1,2,0:T(8,128)}), f32[32,1024,8]{1,2,0:T(8,128)S(1)}, u32[]{:S(2)}, u32[]{:S(2)}) %all-to-all-start.1) | async-done | bytes 1048608 | tf_op jit(solution)/shard_map/all_to_all | solution.py:31
  171.7 47.3 %all-reduce.3.cloned.1.call-done = f32[1024,1024]{0,1:T(8,128)} async-done(((f32[1024,1024]{0,1:T(8,128)}), f32[1024,1024]{0,1:T(8,128)}) %all-reduce.3.cloned.1.call-update) | async-done | bytes 4194320 | tf_op jit(solution)/shard_map/psum | solution.py:47
  219.0 4.8 select_add_fusion
  223.8 5.5 copy.47
  229.3 4.5 fusion.3
  233.8 2.0 copy-done.3
  235.7 11.7 %cholesky.222 = f32[128,128]{1,0:T(8,128)S(1)} custom-call(f32[128,128]{1,0:T(8,128)S(1)} %cholesky.577), custom_call_target="Cholesky" | custom-call | tf_op jit(solution)/shard_map/jit(cholesky)/cholesky | solution.py:52
  247.6 9.8 %custom-call.66 = f32[1,128,128]{1,2,0:T(8,128)S(1)} custom-call(f32[1,128,128]{2,1,0:T(8,128)S(1)} %get-tuple-element.49), custom_call_target="InvertDiagBlocksLowerTriangular" | custom-call | tf_op jit(solution)/shard_map/jit(cholesky)/cholesky | solution.py:52
  257.4 1.5 fusion.20
  259.1 1.6 convolution_subtract_fusion
  260.7 11.7 %cholesky.243 = f32[128,128]{1,0:T(8,128)S(1)} custom-call(f32[128,128]{1,0:T(8,128)S(1)} %cholesky.581), custom_call_target="Cholesky" | custom-call | tf_op jit(solution)/shard_map/jit(cholesky)/cholesky | solution.py:52
  272.8 2.5 cholesky.254
  275.3 9.8 %custom-call.67 = f32[1,128,128]{1,2,0:T(8,128)S(1)} custom-call(f32[1,128,128]{2,1,0:T(8,128)S(1)} %get-tuple-element.47), custom_call_target="InvertDiagBlocksLowerTriangular" | custom-call | tf_op jit(solution)/shard_map/jit(cholesky)/cholesky | solution.py:52
  286.6 1.3 convolution_dynamic-update-slice_fusion
  287.9 2.7 convolution_subtract_fusion.1
  290.6 11.7 %cholesky.466 = f32[128,128]{1,0:T(8,128)S(1)} custom-call(f32[128,128]{1,0:T(8,128)S(1)} %cholesky.586), custom_call_target="Cholesky" | custom-call | tf_op jit(solution)/shard_map/jit(cholesky)/cholesky | solution.py:52
  303.1 9.8 %custom-call.68 = f32[1,128,128]{1,2,0:T(8,128)S(1)} custom-call(f32[1,128,128]{2,1,0:T(8,128)S(1)} %get-tuple-element.45), custom_call_target="InvertDiagBlocksLowerTriangular" | custom-call | tf_op jit(solution)/shard_map/jit(cholesky)/cholesky | solution.py:52
  312.9 1.2 convolution_dynamic-update-slice_fusion.1
  314.1 3.5 convolution_subtract_fusion.2
  317.7 11.7 %cholesky.485 = f32[128,128]{1,0:T(8,128)S(1)} custom-call(f32[128,128]{1,0:T(8,128)S(1)} %cholesky.591), custom_call_target="Cholesky" | custom-call | tf_op jit(solution)/shard_map/jit(cholesky)/cholesky | solution.py:52
  330.2 9.8 %custom-call.69 = f32[1,128,128]{1,2,0:T(8,128)S(1)} custom-call(f32[1,128,128]{2,1,0:T(8,128)S(1)} %get-tuple-element.43), custom_call_target="InvertDiagBlocksLowerTriangular" | custom-call | tf_op jit(solution)/shard_map/jit(cholesky)/cholesky | solution.py:52
  341.1 3.1 convolution_subtract_fusion.3
  344.3 11.9 %cholesky.504 = f32[128,128]{1,0:T(8,128)S(1)} custom-call(f32[128,128]{1,0:T(8,128)S(1)} %cholesky.596), custom_call_target="Cholesky" | custom-call | tf_op jit(solution)/shard_map/jit(cholesky)/cholesky | solution.py:52
  356.9 9.8 %custom-call.70 = f32[1,128,128]{1,2,0:T(8,128)S(1)} custom-call(f32[1,128,128]{2,1,0:T(8,128)S(1)} %get-tuple-element.41), custom_call_target="InvertDiagBlocksLowerTriangular" | custom-call | tf_op jit(solution)/shard_map/jit(cholesky)/cholesky | solution.py:52
  367.9 3.1 convolution_subtract_fusion.4
  371.0 11.7 %cholesky.524 = f32[128,128]{1,0:T(8,128)S(1)} custom-call(f32[128,128]{1,0:T(8,128)S(1)} %cholesky.601), custom_call_target="Cholesky" | custom-call | tf_op jit(solution)/shard_map/jit(cholesky)/cholesky | solution.py:52
  383.5 9.8 %custom-call.71 = f32[1,128,128]{1,2,0:T(8,128)S(1)} custom-call(f32[1,128,128]{2,1,0:T(8,128)S(1)} %get-tuple-element.39), custom_call_target="InvertDiagBlocksLowerTriangular" | custom-call | tf_op jit(solution)/shard_map/jit(cholesky)/cholesky | solution.py:52
  394.3 2.9 convolution_subtract_fusion.5
  397.2 11.7 %cholesky.544 = f32[128,128]{1,0:T(8,128)S(1)} custom-call(f32[128,128]{1,0:T(8,128)S(1)} %cholesky.606), custom_call_target="Cholesky" | custom-call | tf_op jit(solution)/shard_map/jit(cholesky)/cholesky | solution.py:52
  409.6 9.8 %custom-call.72 = f32[1,128,128]{1,2,0:T(8,128)S(1)} custom-call(f32[1,128,128]{2,1,0:T(8,128)S(1)} %get-tuple-element.37), custom_call_target="InvertDiagBlocksLowerTriangular" | custom-call | tf_op jit(solution)/shard_map/jit(cholesky)/cholesky | solution.py:52
  420.4 2.1 convolution_subtract_fusion.6
  422.5 11.7 %cholesky.562 = f32[128,128]{1,0:T(8,128)S(1)} custom-call(f32[128,128]{1,0:T(8,128)S(1)} %convolution_subtract_fusion.6), custom_call_target="Cholesky" | custom-call | tf_op jit(solution)/shard_map/jit(cholesky)/cholesky | solution.py:52
  444.4 4.9 select_select_fusion
  449.3 24.0 %while.1 = (s32[]{:T(128)}, f32[1024,1024]{0,1:T(8,128)}, s32[8,2]{0,1:T(2,128)S(1)}, f32[8,128,128]{2,1,0:T(8,128)S(1)}, s32[]{:T(128)}) while((s32[]{:T(128)}, f32[1024,1024]{0,1:T(8,128)}, s32[8,2]{0,1:T(2,128)S(1)}, f32[8,128,128]{2,1,0:T(8,128)S(1)}, s32[]{:T(128)}) %tuple.57), condition=%wide.while_cond, body=%wide.while_body.sunk | while | flops 2 | bytes 393329 | solution.py:57
  449.9 2.3 dynamic-slice.7
  452.9 2.3 dynamic-slice.7
  455.9 2.3 dynamic-slice.7
  458.9 2.3 dynamic-slice.7
  461.9 2.3 dynamic-slice.7
  464.9 2.3 dynamic-slice.7
  467.9 2.3 dynamic-slice.7
  470.9 2.2 dynamic-slice.7
  473.2 79.0 %custom-call.73 = f32[8,128,128]{1,2,0:T(8,128)S(1)} custom-call(f32[8,128,128]{2,1,0:T(8,128)S(1)} %get-tuple-element.9), custom_call_target="InvertDiagBlocksLowerTriangular" | custom-call | tf_op jit(solution)/shard_map/jit(_cho_solve)/triangular_solve | solution.py:57
  556.2 1.2 convolution_subtract_fusion.13
  557.6 1.3 convolution_subtract_fusion.12
  559.0 1.3 convolution_subtract_fusion.20
  560.5 1.4 convolution_subtract_fusion.19
  564.9 1.2 convolution_subtract_fusion.9
  566.4 1.3 convolution_subtract_fusion.8
  567.9 1.4 convolution_subtract_fusion.7
  569.6 1.4 convolution_subtract_fusion.18
  571.3 1.5 convolution_subtract_fusion.17
  573.2 22.9 %all_to_all.16 = f32[32,1024,8]{1,2,0:T(8,128)S(1)} all-to-all(f32[32,1024,8]{1,2,0:T(8,128)S(1)} %broadcast_in_dim.7), channel_id=1, replica_groups=mesh['rows'=32,'tgt'=4] {'rows'}, dimensions={0} | all-to-all | bytes 2097152 | tf_op jit(solution)/shard_map/all_to_all | solution.py:15
  596.1 1.3 copy.64
  597.4 36.5 %fusion.10 = f32[2048,256]{1,0:T(8,128)} fusion(f32[2048,256]{1,0:T(8,128)} %param.7, f32[2048,1024]{1,0:T(8,128)} %copy-done.2, f32[1024]{0:T(1024)S(1)} %copy-done.5, f32[32,1024,8]{1,2,0:T(8,128)S(1)} %all_to_all.16), kind=kOutput, calls=%fused_computation.18 | convolution fusion | flops 6447169536 | bytes 13635584 | tf_op jit(solution)/shard_map/dot_general | solution.py:59
  (135 shorter events, 30.5 us)
Async XLA Ops:
  7.2 31.8 %copy-start = (bf16[512,1024]{1,0:T(8,128)(2,1)S(1)}, bf16[512,1024]{1,0:T(8,128)(2,1)}, u32[]{:S(2)}) copy-start(bf16[512,1024]{1,0:T(8,128)(2,1)} %param.5) | copy-start | bytes 3145732
  7.2 211.8 %all-reduce.3.cloned.1.call-start = ((), (), s32[]{:S(2)}) async-start(), calls=%async_computation.3 | async-start | bytes 8388608 | tf_op jit(solution)/shard_map/psum | solution.py:47
  38.9 5.6 copy-start.5
  41.3 3.2 copy-start.2
  100.8 1.6 copy-start.4
  144.8 26.8 %all-to-all-start.1 = ((f32[32,1024,8]{1,2,0:T(8,128)}), f32[32,1024,8]{1,2,0:T(8,128)S(1)}, u32[]{:S(2)}, u32[]{:S(2)}) async-start(f32[32,1024,8]{1,2,0:T(8,128)} %fusion.11), calls=%async_computation.1 | async-start | bytes 2097152 | tf_op jit(solution)/shard_map/all_to_all | solution.py:31
  233.8 2.0 copy-start.3
  597.4 36.5 %copy-start.1 = (bf16[512,1024]{1,0:T(8,128)(2,1)S(1)}, bf16[512,1024]{1,0:T(8,128)(2,1)}, u32[]{:S(2)}) copy-start(bf16[512,1024]{1,0:T(8,128)(2,1)} %param.5) | copy-start | bytes 3145732
Sparse Core Ops, SparseCore 0:
  101.0 117.9 all-reduce.2
where the time goes:
time: 648 us; the launch traced here: 641 us
  other arithmetic  287 us (44%)
  matrix products  158 us (24%)
  waiting for transfers between devices  64.3 us (10%)
  blocking collectives  53 us (8%)
  local copies, waits for them, and re-layouts  48.2 us (7%)
  between operations  19.6 us (3%)
  starting transfers between devices  9.95 us (2%)
    another operation x30, other arithmetic, body(): factor = jnp.linalg.cholesky(gram_matrix)  167 us
    another operation x3, other arithmetic, body(): own_coef = jax.scipy.linalg.cho_solve((factor, True), own_corr)  83.9 us
    all_to_all x2, blocking collectives, from_everyone(): lax.all_to_all(jnp.broadcast_to(value[None], (count, *value.shape)), axis...  53 us
    psum x1, waiting for transfers between devices, body(): gram_matrix = lax.psum(gram_of(feature), 'rows')  47.3 us
    dot_general x1, matrix products, body(): jnp.dot(feature.T, residual, precision=highest, preferred_element_type=jn...  42.3 us
    dot_general x1, matrix products, body(): jnp.dot(feature, coefficients, precision=highest, preferred_element_type=...  36.5 us
    dot_general x1, matrix products, gram_of(): jnp.dot(row_block.T, row_block, precision=lax.Precision.HIGHEST, preferre...  29.3 us
    another operation x14, matrix products, body(): factor = jnp.linalg.cholesky(gram_matrix)  27.2 us
  transfers between devices with their start and end apart: 2, of which 2 were waited for; matrix products, arithmetic and copies ran while one was open for 7% of the time, Pallas kernels for 0%

commit v1 on v0

v1 whole, which is shorter than its diff:
```python
import math

import jax
import jax.numpy as jnp
from jax import lax
from jax.experimental import pallas as pl
from jax.experimental.pallas import tpu as pltpu
from jax.sharding import PartitionSpec as P

F32 = jnp.float32
BF16 = jnp.bfloat16
HIGHEST = lax.Precision.HIGHEST
NB = 128
PB = 16
SIN_PI = (
    3.1415926535362892,
    -5.167712764624528,
    2.5501633189472983,
    -0.5992521978285216,
    0.08205040183240117,
    -0.007028386446239114,
)


def dot(a, b, precision=None):
    return lax.dot_general(
        a, b, (((1,), (0,)), ((), ())), precision=precision, preferred_element_type=F32
    )


def dot_t(a, b, precision=None):
    return lax.dot_general(
        a, b, (((0,), (0,)), ((), ())), precision=precision, preferred_element_type=F32
    )


def split2(x):
    high = x.astype(BF16)
    return high, (x - high.astype(F32)).astype(BF16)


def split3(x):
    high = x.astype(BF16)
    rest = x - high.astype(F32)
    mid = rest.astype(BF16)
    return high, mid, (rest - mid.astype(F32)).astype(BF16)


def features(frames, weights, phases):
    turns = (dot(frames, weights) + phases) * (0.5 / math.pi)
    r = turns - jnp.round(turns)
    s = r * r
    poly = jnp.full_like(s, SIN_PI[-1])
    for coef in SIN_PI[-2::-1]:
        poly = poly * s + coef
    half = poly * r
    scale = math.sqrt(2.0 / weights.shape[1])
    return scale - (2.0 * scale) * (half * half)


def packed_slot(block, blocks):
    if block < blocks // 2:
        return block, 0
    return blocks - 1 - block, (block + 1) * NB


def gram_kernel(frames, weights, phases, out, high, low):
    blocks = out.shape[0] * 2
    h, l = split2(features(frames[...], weights[...], phases[...]))
    high[...] = h
    low[...] = l
    for i in range(blocks):
        rows = slice(i * NB, (i + 1) * NB)
        right = slice(i * NB, blocks * NB)
        g = dot_t(high[:, rows], high[:, right])
        g = g + dot_t(high[:, rows], low[:, right])
        g = g + dot_t(low[:, rows], high[:, right])
        at, col = packed_slot(i, blocks)
        out[at, :, col : col + (blocks - i) * NB] = g


def feature_kernel(frames, weights, phases, residual, high, low, corr):
    h, l = split2(features(frames[...], weights[...], phases[...]))
    high[...] = h
    low[...] = l
    rh, rl = split2(residual[...])
    part = dot_t(h, rh) + dot_t(h, rl) + dot_t(l, rh)

    @pl.when(pl.program_id(0) == 0)
    def _():
        corr[...] = part

    @pl.when(pl.program_id(0) > 0)
    def _():
        corr[...] += part


def invert_block(d):
    lane = lax.broadcasted_iota(jnp.int32, (PB, NB), 1)
    sub = lax.broadcasted_iota(jnp.int32, (PB, NB), 0)
    col_at = lax.broadcasted_iota(jnp.int32, (NB, NB), 1)
    zero = jnp.zeros((PB, NB), F32)
    for k0 in range(0, NB, PB):
        rows = d[k0 : k0 + PB, :]
        cols = [jnp.broadcast_to(rows[:, k0 + j : k0 + j + 1], (PB, NB)) for j in range(PB)]
        lh, lm, ll = split3(jnp.where(lane < k0, -rows, rows))
        left = jnp.concatenate([lh, lh, lm, lm, lh, ll], axis=0)
        x = jnp.where((lane >= k0) & (lane < k0 + PB), jnp.where(lane - k0 == sub, 1.0, 0.0), rows)
        scale = zero
        for k in range(PB):
            c = cols[k]
            p = 1.0 / c[k : k + 1, :]
            m = jnp.where(sub == k, 0.0, c * p)
            scale = jnp.where(sub == k, p, scale)
            for j in range(k + 1, PB):
                cols[j] = cols[j] - m * cols[j][k : k + 1, :]
            x = x - m * x[k : k + 1, :]
        x = x * scale
        xh, xm, xl = split3(x)
        right = jnp.concatenate([xh, xm, xh, xm, xl, xh], axis=0)
        update = dot_t(left, right)
        kept = d[...]
        d[...] = jnp.where((col_at >= k0) & (col_at < k0 + PB), 0.0, kept) - update
        d[k0 : k0 + PB, :] = x


def factor_kernel(pack, panel, inverse, a, d, *, ridge):
    blocks = panel.shape[0]
    size = blocks * NB
    for i in range(blocks):
        at, col = packed_slot(i, blocks)
        a[i, :, i * NB : size] = pack[at, :, col : col + size - i * NB]
        if i > 0:
            a[i, :, : i * NB] = jnp.zeros((NB, i * NB), F32)
            panel[i, :, : i * NB] = jnp.zeros((NB, i * NB), F32)
    eye = jnp.where(
        lax.broadcasted_iota(jnp.int32, (NB, NB), 0) == lax.broadcasted_iota(jnp.int32, (NB, NB), 1),
        ridge,
        0.0,
    ).astype(F32)

    def step(i, _):
        own = pl.ds(pl.multiple_of(i * NB, NB), NB)
        d[...] = a[i, :, own] + eye
        invert_block(d)
        inverse[i] = d[...]

        def eliminate(first):
            panel[i, :, first:] = dot(d[...], a[i, :, first:], HIGHEST)

            def row(j, _):
                left = a[i, :, pl.ds(pl.multiple_of(j * NB, NB), NB)]
                a[j, :, first:] = a[j, :, first:] - dot_t(left, panel[i, :, first:], HIGHEST)
                return 0

            lax.fori_loop(i + 1, blocks, row, 0)

        for part in range(4):
            low = part * (blocks // 4)

            @pl.when((i >= low) & (i < low + blocks // 4))
            def _():
                eliminate(low * NB)

        return 0

    lax.fori_loop(0, blocks, step, 0)


def solve_kernel(panel, inverse, corr, out, c):
    blocks = panel.shape[0]
    c[...] = jnp.zeros_like(c)
    for i in range(blocks):
        rows = slice(i * NB, (i + 1) * NB)
        value = corr[rows, :]
        for j in range(i):
            value = value - dot_t(panel[j, :, rows], c[j * NB : (j + 1) * NB, :], HIGHEST)
        c[rows, :] = value
    for i in range(blocks - 1, -1, -1):
        rows = slice(i * NB, (i + 1) * NB)
        value = dot(inverse[i], c[rows, :], HIGHEST)
        if i < blocks - 1:
            rest = (i + 1) * NB
            value = value - dot(panel[i, :, rest:], out[rest:, :], HIGHEST)
        out[rows, :] = value


def update_kernel(high, low, coef, residual, out):
    wh, wl = split2(coef[...])
    h = high[...]
    out[...] = residual[...] - (dot(h, wh) + dot(h, wl) + dot(low[...], wh))


def params(**kw):
    return pltpu.CompilerParams(vmem_limit_bytes=56 * 1024 * 1024, **kw)


def factor_call(pack, ridge):
    blocks = pack.shape[0] * 2
    return pl.pallas_call(
        lambda *refs: factor_kernel(*refs, ridge=ridge),
        out_shape=(
            jax.ShapeDtypeStruct((blocks, NB, blocks * NB), F32),
            jax.ShapeDtypeStruct((blocks, NB, NB), F32),
        ),
        scratch_shapes=[
            pltpu.VMEM((blocks, NB, blocks * NB), F32),
            pltpu.VMEM((NB, NB), F32),
        ],
        compiler_params=params(),
        name="factor",
    )(pack)


def solve_call(panel, inverse, corr):
    return pl.pallas_call(
        solve_kernel,
        out_shape=jax.ShapeDtypeStruct(corr.shape, F32),
        scratch_shapes=[pltpu.VMEM(corr.shape, F32)],
        compiler_params=params(),
        name="solve",
    )(panel, inverse, corr)


def gram_call(frames, weights, phases):
    rows = frames.shape[0]
    feat = weights.shape[1]
    blocks = feat // NB
    return pl.pallas_call(
        gram_kernel,
        out_shape=jax.ShapeDtypeStruct((blocks // 2, NB, feat + NB), F32),
        scratch_shapes=[pltpu.VMEM((rows, feat), BF16), pltpu.VMEM((rows, feat), BF16)],
        compiler_params=params(),
        name="gram",
    )(frames, weights, phases)


def feature_call(frames, weights, phases, residual, tile=256):
    rows, din = frames.shape
    feat = weights.shape[1]
    cols = residual.shape[1]
    return pl.pallas_call(
        feature_kernel,
        grid=(rows // tile,),
        in_specs=[
            pl.BlockSpec((tile, din), lambda i: (i, 0)),
            pl.BlockSpec((din, feat), lambda i: (0, 0)),
            pl.BlockSpec((1, feat), lambda i: (0, 0)),
            pl.BlockSpec((tile, cols), lambda i: (i, 0)),
        ],
        out_specs=[
            pl.BlockSpec((tile, feat), lambda i: (i, 0)),
            pl.BlockSpec((tile, feat), lambda i: (i, 0)),
            pl.BlockSpec((feat, cols), lambda i: (0, 0)),
        ],
        out_shape=[
            jax.ShapeDtypeStruct((rows, feat), BF16),
            jax.ShapeDtypeStruct((rows, feat), BF16),
            jax.ShapeDtypeStruct((feat, cols), F32),
        ],
        compiler_params=params(dimension_semantics=("arbitrary",)),
        name="features",
    )(frames, weights, phases, residual)


def update_call(high, low, coef, residual, tile=256):
    rows, feat = high.shape
    cols = residual.shape[1]
    return pl.pallas_call(
        update_kernel,
        grid=(rows // tile,),
        in_specs=[
            pl.BlockSpec((tile, feat), lambda i: (i, 0)),
            pl.BlockSpec((tile, feat), lambda i: (i, 0)),
            pl.BlockSpec((feat, cols), lambda i: (0, 0)),
            pl.BlockSpec((tile, cols), lambda i: (i, 0)),
        ],
        out_specs=pl.BlockSpec((tile, cols), lambda i: (i, 0)),
        out_shape=jax.ShapeDtypeStruct((rows, cols), F32),
        compiler_params=params(dimension_semantics=("arbitrary",)),
        name="update",
    )(high, low, coef, residual)


def body(frames, weights, phases, residual):
    rows_here = frames.shape[0]
    feature_count = weights.shape[1]
    ridge = 0.1 * rows_here * lax.axis_size("rows") / feature_count
    phases = phases[None, :]
    gathered = lax.all_gather(frames, "tgt", axis=1, tiled=True)
    share = rows_here // lax.axis_size("tgt")
    own = lax.dynamic_slice_in_dim(gathered, lax.axis_index("tgt") * share, share, 0)
    pack = lax.psum(gram_call(own, weights, phases), ("rows", "tgt"))
    high, low, corr = feature_call(gathered, weights, phases, residual)
    corr = lax.psum(corr, "rows")
    panel, inverse = factor_call(pack, ridge)
    coefficients = solve_call(panel, inverse, corr)
    residual_next = update_call(high, low, coefficients, residual)
    return (residual_next, coefficients)


def solution(mesh):
    return jax.shard_map(
        body,
        mesh=mesh,
        in_specs=(P("rows", "tgt"), P(), P(), P("rows", "tgt")),
        out_specs=(P("rows", "tgt"), P(None, "tgt")),
        check_vma=False,
    )
```

time: 648 us -> 345 us (0.53); the launches traced: 641 us -> 345 us
  other arithmetic: 287 us -> 0 us
  waiting for transfers between devices: 64.3 us -> 236 us
  matrix products: 158 us -> 0 us
  Pallas kernels: 0 us -> 93.7 us
  blocking collectives: 53 us -> 0 us
  local copies, waits for them, and re-layouts: 48.2 us -> 1.87 us
  starting transfers between devices: 9.95 us -> 0.12 us
    another operation x33 -> x0, other arithmetic: 251 us -> none  [the longest x30 167 us: body(): factor = jnp.linalg.cholesky(gram_matrix)]
    psum x1 -> x2, waiting for transfers between devices: 47.3 us -> 197 us  [the longest x1 139 us: body(): pack = lax.psum(gram_call(own, weights, phases), ('rows', 'tgt'))]
    dot_general x4 -> x0, matrix products: 111 us -> none  [the longest x1 42.3 us: body(): jnp.dot(feature.T, residual, precision=highest, preferred_element_type=jn...]
    pallas_call x0 -> x5, Pallas kernels: none -> 93.7 us  [the longest x1 49.6 us: factor_call(): pl.pallas_call(lambda *refs: factor_kernel(*refs, ridge=ridge), out_shape...]
    all_to_all x2 -> x0, blocking collectives: 53 us -> none  [from_everyone(): lax.all_to_all(jnp.broadcast_to(value[None], (count, *value.shape)), axis...]
    another operation x44 -> x0, matrix products: 47.7 us -> none  [the longest x14 27.2 us: body(): factor = jnp.linalg.cholesky(gram_matrix)]
    all_gather x0 -> x1, waiting for transfers between devices: none -> 37.5 us  [body(): gathered = lax.all_gather(frames, 'tgt', axis=1, tiled=True)]
    another operation x70 -> x0, local copies, waits for them, and re-layouts: 32.8 us -> none
  transfers between devices with their start and end apart: 2 -> 3, of which waited for: 2 -> 3; matrix products, arithmetic and copies ran while one was open for 7% -> 0% of each run, Pallas kernels for 0% -> 19%
where the time goes in v1:
time: 345 us
  waiting for transfers between devices  236 us (68%)
  Pallas kernels  93.7 us (27%)
  between operations  13.8 us (4%)
    psum x1, waiting for transfers between devices, body(): pack = lax.psum(gram_call(own, weights, phases), ('rows', 'tgt'))  139 us
    psum x1, waiting for transfers between devices, body(): corr = lax.psum(corr, 'rows')  58.7 us
    pallas_call x1, Pallas kernels, factor_call(): pl.pallas_call(lambda *refs: factor_kernel(*refs, ridge=ridge), out_shape...  49.6 us
    all_gather x1, waiting for transfers between devices, body(): gathered = lax.all_gather(frames, 'tgt', axis=1, tiled=True)  37.5 us
    pallas_call x1, Pallas kernels, feature_call(): pl.pallas_call(feature_kernel, grid=(rows // tile,), in_specs=[pl.BlockSp...  15.3 us
    pallas_call x1, Pallas kernels, solve_call(): pl.pallas_call(solve_kernel, out_shape=jax.ShapeDtypeStruct(corr.shape, F...  11.8 us
    pallas_call x1, Pallas kernels, update_call(): pl.pallas_call(update_kernel, grid=(rows // tile,), in_specs=[pl.BlockSpe...  10 us
    pallas_call x1, Pallas kernels, gram_call(): pl.pallas_call(gram_kernel, out_shape=jax.ShapeDtypeStruct((blocks // 2,...  7.06 us
  transfers between devices with their start and end apart: 3, of which 3 were waited for; matrix products, arithmetic and copies ran while one was open for 0% of the time, Pallas kernels for 19%

profile of v1, /device:TPU:1, one launch (start us, length us, event | category | flops | bytes accessed | tf_op | source)
XLA Modules:
  0.0 345.0 jit_solution(17447835104232784401)
XLA Ops:
  7.2 0.0 all-gather.2.cloned.1.call-start
  7.2 0.7 all-gather.2.cloned.1.call-update
  7.9 0.0 all-reduce.3.cloned.1.call-start
  7.9 37.5 %all-gather.2.cloned.1.call-done.frames = bf16[2048,512]{1,0:T(8,128)(2,1)} async-done(((bf16[2048,128]{1,0:T(8,128)(2,1)}), bf16[2048,512]{1,0:T(8,128)(2,1)}) %all-gather.2.cloned.1.call-update) | async-done | bytes 2097168 | tf_op jit(solution)/shard_map/all_gather | solution.py:290
  45.4 1.9 constant_dynamic-slice_fusion.frames
  47.3 7.1 %gram.1 = f32[4,128,1152]{2,1,0:T(8,128)} custom-call(bf16[512,512]{1,0:T(8,128)(2,1)} %constant_dynamic-slice_fusion.frames, bf16[512,1024]{1,0:T(8,128)(2,1)} %weights.3, f32[1,1024]{1,0:T(1,128)} %bitcast.1), custom_call_target="tpu_custom_call" | custom-call | tf_op jit(solution)/shard_map/gram/pallas_call | solution.py:229
  54.3 0.0 all-reduce.3.cloned.1.call-update
  54.4 0.0 all-reduce.5.cloned.1.call-start
  54.4 15.3 %features.1 = (bf16[2048,1024]{1,0:T(8,128)(2,1)}, bf16[2048,1024]{1,0:T(8,128)(2,1)}, f32[1024,256]{1,0:T(8,128)}) custom-call(bf16[2048,512]{1,0:T(8,128)(2,1)} %all-gather.2.cloned.1.call-done.frames, bf16[512,1024]{1,0:T(8,128)(2,1)} %weights.3, f32[1,1024]{1,0:T(1,128)} %bitcast.2, f32[2048,256]{1,0:T(8,128)} %residual.3), custom_call_target="tpu_custom_call" | custom-call | tf_op jit(solution)/shard_map/features/pallas_call | solution.py:242
  69.8 0.0 all-reduce.5.cloned.1.call-update
  69.8 138.7 %all-reduce.3.cloned.1.call-done.refs_0_ = f32[4,128,1152]{2,1,0:T(8,128)} async-done(((f32[4,128,1152]{2,1,0:T(8,128)}), f32[4,128,1152]{2,1,0:T(8,128)}) %all-reduce.3.cloned.1.call-update) | async-done | bytes 2359312 | tf_op jit(solution)/shard_map/psum | solution.py:293
  208.4 49.6 %factor.1 = (f32[8,128,1024]{2,1,0:T(8,128)}, f32[8,128,128]{2,1,0:T(8,128)}) custom-call(f32[4,128,1152]{2,1,0:T(8,128)} %all-reduce.3.cloned.1.call-done.refs_0_), custom_call_target="tpu_custom_call" | custom-call | tf_op jit(solution)/shard_map/factor/pallas_call | solution.py:200
  258.0 58.7 %all-reduce.5.cloned.1.call-done.corr = f32[1024,256]{1,0:T(8,128)} async-done(((f32[1024,256]{1,0:T(8,128)}), f32[1024,256]{1,0:T(8,128)}) %all-reduce.5.cloned.1.call-update) | async-done | bytes 1048592 | tf_op jit(solution)/shard_map/psum | solution.py:295
  316.7 11.8 %solve.1.coef = f32[1024,256]{1,0:T(8,128)} custom-call(f32[8,128,1024]{2,1,0:T(8,128)} %get-tuple-element.9.panel, f32[8,128,128]{2,1,0:T(8,128)} %get-tuple-element.10.inverse, f32[1024,256]{1,0:T(8,128)} %all-reduce.5.cloned.1.call-done.corr), custom_call_target="tpu_custom_call" | custom-call | tf_op jit(solution)/shard_map/solve/pallas_call | solution.py:216
  328.5 10.0 %update.1 = f32[2048,256]{1,0:T(8,128)} custom-call(bf16[2048,1024]{1,0:T(8,128)(2,1)} %get-tuple-element.7.high, bf16[2048,1024]{1,0:T(8,128)(2,1)} %get-tuple-element.8.low, f32[1024,256]{1,0:T(8,128)} %solve.1.coef, f32[2048,256]{1,0:T(8,128)} %residual.3), custom_call_target="tpu_custom_call" | custom-call | tf_op jit(solution)/shard_map/update/pallas_call | solution.py:269
Async XLA Ops:
  7.2 38.2 %all-gather.2.cloned.1.call-start = ((), (), s32[]{:S(2)}) async-start(), calls=%async_computation | async-start | bytes 2621440 | tf_op jit(solution)/shard_map/all_gather | solution.py:290
  7.9 200.5 %all-reduce.3.cloned.1.call-start = ((), (), s32[]{:S(2)}) async-start(), calls=%async_computation.1 | async-start | bytes 4718592 | tf_op jit(solution)/shard_map/psum | solution.py:293
  54.4 262.3 %all-reduce.5.cloned.1.call-start = ((), (), s32[]{:S(2)}) async-start(), calls=%async_computation.2 | async-start | bytes 2097152 | tf_op jit(solution)/shard_map/psum | solution.py:295
Sparse Core Ops, SparseCore 0:
  9.6 35.7 all-gather.1
  54.5 153.9 all-reduce.2
  212.3 104.3 all-reduce.4

commit v2 on v1

--- a/solution.py
+++ b/solution.py
@@ -66,7 +66,8 @@
 
 def gram_kernel(frames, weights, phases, out, high, low):
     blocks = out.shape[0] * 2
-    h, l = split2(features(frames[...], weights[...], phases[...]))
+    slabs = jnp.concatenate([frames[i] for i in range(frames.shape[0])], axis=1)
+    h, l = split2(features(slabs, weights[...], phases[...]))
     high[...] = h
     low[...] = l
     for i in range(blocks):
@@ -79,8 +80,10 @@
         out[at, :, col : col + (blocks - i) * NB] = g
 
 
-def feature_kernel(frames, weights, phases, residual, high, low, corr):
-    h, l = split2(features(frames[...], weights[...], phases[...]))
+def feature_kernel(order, own, left, right, far, weights, phases, residual, high, low, corr):
+    slabs = jnp.concatenate([own[...], left[...], right[...], far[...]], axis=1)
+    sorted_weights = jnp.concatenate([weights[order[i]] for i in range(4)], axis=0)
+    h, l = split2(features(slabs, sorted_weights, phases[...]))
     high[...] = h
     low[...] = l
     rh, rl = split2(residual[...])
@@ -124,12 +127,25 @@
         d[k0 : k0 + PB, :] = x
 
 
-def factor_kernel(pack, panel, inverse, a, d, *, ridge):
+def factor_kernel(core, mine, other, panel, inverse, a, d, *, ridge):
     blocks = panel.shape[0]
     size = blocks * NB
+    quarter = blocks // 4
+
+    def unpack(halves):
+        for i in range(blocks):
+            at, col = packed_slot(i, blocks)
+            a[i, :, i * NB : size] = halves[at // quarter][at % quarter, :, col : col + size - i * NB]
+
+    @pl.when(core[0] == 0)
+    def _():
+        unpack((mine, other))
+
+    @pl.when(core[0] != 0)
+    def _():
+        unpack((other, mine))
+
     for i in range(blocks):
-        at, col = packed_slot(i, blocks)
-        a[i, :, i * NB : size] = pack[at, :, col : col + size - i * NB]
         if i > 0:
             a[i, :, : i * NB] = jnp.zeros((NB, i * NB), F32)
             panel[i, :, : i * NB] = jnp.zeros((NB, i * NB), F32)
@@ -195,10 +211,12 @@
     return pltpu.CompilerParams(vmem_limit_bytes=56 * 1024 * 1024, **kw)
 
 
-def factor_call(pack, ridge):
-    blocks = pack.shape[0] * 2
+def factor_call(core, mine, other, ridge):
+    blocks = mine.shape[0] * 4
+    vmem = pl.BlockSpec(memory_space=pltpu.VMEM)
     return pl.pallas_call(
         lambda *refs: factor_kernel(*refs, ridge=ridge),
+        in_specs=[pl.BlockSpec(memory_space=pltpu.SMEM), vmem, vmem],
         out_shape=(
             jax.ShapeDtypeStruct((blocks, NB, blocks * NB), F32),
             jax.ShapeDtypeStruct((blocks, NB, NB), F32),
@@ -209,7 +227,7 @@
         ],
         compiler_params=params(),
         name="factor",
-    )(pack)
+    )(core, mine, other)
 
 
 def solve_call(panel, inverse, corr):
@@ -223,7 +241,7 @@
 
 
 def gram_call(frames, weights, phases):
-    rows = frames.shape[0]
+    rows = frames.shape[1]
     feat = weights.shape[1]
     blocks = feat // NB
     return pl.pallas_call(
@@ -235,16 +253,17 @@
     )(frames, weights, phases)
 
 
-def feature_call(frames, weights, phases, residual, tile=256):
-    rows, din = frames.shape
+def feature_call(order, slabs, weights, phases, residual, tile=256):
+    rows, width = slabs[0].shape
     feat = weights.shape[1]
     cols = residual.shape[1]
     return pl.pallas_call(
         feature_kernel,
         grid=(rows // tile,),
         in_specs=[
-            pl.BlockSpec((tile, din), lambda i: (i, 0)),
-            pl.BlockSpec((din, feat), lambda i: (0, 0)),
+            pl.BlockSpec(memory_space=pltpu.SMEM),
+            *[pl.BlockSpec((tile, width), lambda i: (i, 0))] * 4,
+            pl.BlockSpec((4, width, feat), lambda i: (0, 0, 0)),
             pl.BlockSpec((1, feat), lambda i: (0, 0)),
             pl.BlockSpec((tile, cols), lambda i: (i, 0)),
         ],
@@ -260,7 +279,7 @@
         ],
         compiler_params=params(dimension_semantics=("arbitrary",)),
         name="features",
-    )(frames, weights, phases, residual)
+    )(order, *slabs, weights.reshape(4, width, feat), phases, residual)
 
 
 def update_call(high, low, coef, residual, tile=256):
@@ -282,28 +301,77 @@
     )(high, low, coef, residual)
 
 
+UP = [(i, (i + 1) % 4) for i in range(4)]
+DOWN = [(i, (i - 1) % 4) for i in range(4)]
+SWAP = [(0, 1), (1, 0)]
+
+
+def exchange(parts, axes):
+    return lax.all_to_all(parts, axes, 0, 0, tiled=True)
+
+
+def to_everyone(value, axes):
+    return exchange(jnp.broadcast_to(value[None], (lax.axis_size(axes), *value.shape)), axes)
+
+
+def ring_slabs(own):
+    left = lax.ppermute(own, "tgt", UP)
+    right = lax.ppermute(own, "tgt", DOWN)
+    half = own.shape[0] // 2
+    far_top = lax.ppermute(left[:half], "tgt", UP)
+    far_bottom = lax.ppermute(right[half:], "tgt", DOWN)
+    return left, right, jnp.concatenate([far_top, far_bottom], axis=0)
+
+
+def summed_gram(pack, core):
+    halves = pack.reshape(2, -1, *pack.shape[1:])
+    mine = lax.dynamic_index_in_dim(halves, core, 0, keepdims=False)
+    other = lax.dynamic_index_in_dim(halves, 1 - core, 0, keepdims=False)
+    mine = mine + lax.ppermute(other, "core", SWAP)
+    chips = ("y", "z", "tgt")
+    count = lax.axis_size(chips)
+    parts = mine.reshape(count, -1, mine.shape[-1])
+    piece = jnp.sum(exchange(parts, chips), axis=0)
+    mine = to_everyone(piece, chips).reshape(mine.shape)
+    return mine, lax.ppermute(mine, "core", SWAP)
+
+
+def summed_corr(corr):
+    plane = ("y", "z")
+    count = lax.axis_size(plane)
+    piece = jnp.sum(exchange(corr.reshape(count, -1, corr.shape[-1]), plane), axis=0)
+    piece = piece + lax.ppermute(piece, "core", SWAP)
+    return to_everyone(piece, plane).reshape(corr.shape)
+
+
 def body(frames, weights, phases, residual):
     rows_here = frames.shape[0]
     feature_count = weights.shape[1]
-    ridge = 0.1 * rows_here * lax.axis_size("rows") / feature_count
+    ridge = 0.1 * rows_here * lax.axis_size(("y", "z", "core")) / feature_count
     phases = phases[None, :]
-    gathered = lax.all_gather(frames, "tgt", axis=1, tiled=True)
-    share = rows_here // lax.axis_size("tgt")
-    own = lax.dynamic_slice_in_dim(gathered, lax.axis_index("tgt") * share, share, 0)
-    pack = lax.psum(gram_call(own, weights, phases), ("rows", "tgt"))
-    high, low, corr = feature_call(gathered, weights, phases, residual)
-    corr = lax.psum(corr, "rows")
-    panel, inverse = factor_call(pack, ridge)
+    core = lax.axis_index("core")
+    at = lax.axis_index("tgt")
+    whole_rows = exchange(frames.reshape(4, rows_here // 4, -1), "tgt")
+    whole_rows, own = lax.optimization_barrier((whole_rows, frames))
+    slabs = (own, *ring_slabs(own))
+    pack = gram_call(whole_rows, weights, phases)
+    mine, other = summed_gram(pack, core)
+    order = jnp.stack([at, at + 3, at + 1, at + 2]) % 4
+    high, low, corr = feature_call(order, slabs, weights, phases, residual)
+    corr = summed_corr(corr)
+    panel, inverse = factor_call(core[None], mine, other, ridge)
     coefficients = solve_call(panel, inverse, corr)
     residual_next = update_call(high, low, coefficients, residual)
     return (residual_next, coefficients)
 
 
 def solution(mesh):
+    rows = ("y", "z", "core")
+    mesh = jax.sharding.Mesh(mesh.devices.reshape(4, 4, 2, 4), (*rows, "tgt"))
     return jax.shard_map(
         body,
         mesh=mesh,
-        in_specs=(P("rows", "tgt"), P(), P(), P("rows", "tgt")),
-        out_specs=(P("rows", "tgt"), P(None, "tgt")),
+        in_specs=(P(rows, "tgt"), P(), P(), P(rows, "tgt")),
+        out_specs=(P(rows, "tgt"), P(None, "tgt")),
         check_vma=False,
     )

time: 345 us -> 218 us (0.63)
  waiting for transfers between devices: 236 us -> 49.8 us
  starting transfers between devices: 0.12 us -> 34.5 us
  blocking collectives: 0 us -> 28.7 us
  between operations: 13.8 us -> 0.76 us
  local copies, waits for them, and re-layouts: 1.87 us -> 6.3 us
    psum x2 -> x0, waiting for transfers between devices: 197 us -> none  [the longest x1 139 us: body(): pack = lax.psum(gram_call(own, weights, phases), ('rows', 'tgt'))]
    all_gather x1 -> x0, waiting for transfers between devices: 37.5 us -> none  [body(): gathered = lax.all_gather(frames, 'tgt', axis=1, tiled=True)]
    ppermute x0 -> x7, waiting for transfers between devices: none -> 31.4 us  [the longest x1 21.5 us: ring_slabs(): right = lax.ppermute(own, 'tgt', DOWN)]
    all_to_all x0 -> x1, blocking collectives: none -> 28.7 us  [exchange(): return lax.all_to_all(parts, axes, 0, 0, tiled=True)]
    all_to_all x0 -> x4, starting transfers between devices: none -> 19.5 us  [exchange(): return lax.all_to_all(parts, axes, 0, 0, tiled=True)]
    all_to_all x0 -> x4, waiting for transfers between devices: none -> 18.4 us  [exchange(): return lax.all_to_all(parts, axes, 0, 0, tiled=True)]
    ppermute x0 -> x7, starting transfers between devices: none -> 15 us  [the longest x1 4.59 us: summed_corr(): piece = piece + lax.ppermute(piece, 'core', SWAP)]
  transfers between devices with their start and end apart: 3 -> 11, of which waited for: 3 -> 7; matrix products, arithmetic and copies ran while one was open for 0% -> 1% of each run, Pallas kernels for 19% -> 30%
where the time goes in v2:
time: 218 us; the launch traced here: 217 us
  Pallas kernels  94 us (43%)
  waiting for transfers between devices  49.8 us (23%)
  starting transfers between devices  34.5 us (16%)
  blocking collectives  28.7 us (13%)
  local copies, waits for them, and re-layouts  6.3 us (3%)
  other arithmetic  3.18 us (1%)
    pallas_call x1, Pallas kernels, factor_call(): pl.pallas_call(lambda *refs: factor_kernel(*refs, ridge=ridge), in_specs=...  49.5 us
    all_to_all x1, blocking collectives, exchange(): return lax.all_to_all(parts, axes, 0, 0, tiled=True)  28.7 us
    ppermute x1, waiting for transfers between devices, ring_slabs(): right = lax.ppermute(own, 'tgt', DOWN)  21.5 us
    all_to_all x4, starting transfers between devices, exchange(): return lax.all_to_all(parts, axes, 0, 0, tiled=True)  19.5 us
    all_to_all x4, waiting for transfers between devices, exchange(): return lax.all_to_all(parts, axes, 0, 0, tiled=True)  18.4 us
    pallas_call x1, Pallas kernels, feature_call(): pl.pallas_call(feature_kernel, grid=(rows // tile,), in_specs=[pl.BlockSp...  15.7 us
    pallas_call x1, Pallas kernels, solve_call(): pl.pallas_call(solve_kernel, out_shape=jax.ShapeDtypeStruct(corr.shape, F...  11.8 us
    pallas_call x1, Pallas kernels, update_call(): pl.pallas_call(update_kernel, grid=(rows // tile,), in_specs=[pl.BlockSpe...  10 us
  transfers between devices with their start and end apart: 11, of which 7 were waited for; matrix products, arithmetic and copies ran while one was open for 1% of the time, Pallas kernels for 30%

profile of v2, /device:TPU:1, one launch (start us, length us, event | category | flops | bytes accessed | tf_op | source)
XLA Modules:
  0.0 217.2 jit_solution(11690179602142234944)
XLA Ops:
  0.6 4.8 %all-to-all-start = ((bf16[4,512,128]{2,1,0:T(8,128)(2,1)}), bf16[4,512,128]{2,1,0:T(8,128)(2,1)S(1)}, u32[]{:S(2)}, u32[]{:S(2)}) async-start(bf16[4,512,128]{2,1,0:T(8,128)(2,1)} %bitcast.19), calls=%async_computation | async-start | bytes 1048576 | tf_op jit(solution)/shard_map/all_to_all | solution.py:310
  5.5 8.3 %all-to-all-done.frames = bf16[4,512,128]{2,1,0:T(8,128)(2,1)S(1)} async-done(((bf16[4,512,128]{2,1,0:T(8,128)(2,1)}), bf16[4,512,128]{2,1,0:T(8,128)(2,1)S(1)}, u32[]{:S(2)}, u32[]{:S(2)}) %all-to-all-start) | async-done | bytes 524320 | tf_op jit(solution)/shard_map/all_to_all | solution.py:310
  13.8 0.0 copy-start.4
  13.8 0.8 copy-done.4
  14.6 7.0 %gram.1 = f32[4,128,1152]{2,1,0:T(8,128)} custom-call(bf16[4,512,128]{2,1,0:T(8,128)(2,1)} %copy-done.4, bf16[512,1024]{1,0:T(8,128)(2,1)} %weights.1, f32[1,1024]{1,0:T(1,128)} %bitcast.21), custom_call_target="tpu_custom_call" | custom-call | tf_op jit(solution)/shard_map/gram/pallas_call | solution.py:247
  21.6 0.0 copy-start
  21.6 1.5 dynamic-slice_bitcast_fusion
  23.1 2.2 %collective-permute-start.4 = (f32[2,128,1152]{2,1,0:T(8,128)S(1)}, f32[2,128,1152]{2,1,0:T(8,128)}, u32[]{:S(2)}, u32[]{:S(2)}) collective-permute-start(f32[2,128,1152]{2,1,0:T(8,128)S(1)} %dynamic-slice_bitcast_fusion), channel_id=1, source_target_pairs={{0,4},{4,0},{1,5},{5,1},{2,6},{6,2},{3,7},{7,3},{8,12},{12,8},{9,1... | collective-permute-start | bytes 3538952 | tf_op jit(solution)/shard_map/ppermute | solution.py:330
  25.3 2.6 %collective-permute-done.4 = f32[2,128,1152]{2,1,0:T(8,128)} collective-permute-done((f32[2,128,1152]{2,1,0:T(8,128)S(1)}, f32[2,128,1152]{2,1,0:T(8,128)}, u32[]{:S(2)}, u32[]{:S(2)}) %collective-permute-start.4) | collective-permute-done | bytes 1179680 | tf_op jit(solution)/shard_map/ppermute | solution.py:330
  27.9 0.0 copy-done
  27.9 1.4 bitcast_add_fusion
  29.3 0.3 reshape.30
  29.7 28.7 %all_to_all.25 = f32[64,4,1152]{2,1,0:T(4,128)S(1)} all-to-all(f32[64,4,1152]{2,1,0:T(4,128)S(1)} %reshape.30), channel_id=1, replica_groups=mesh['y'=4,'z'=4,'core'=2,'tgt'=4] {'y','z','tgt'}, dimensions={0} | all-to-all | bytes 2359296 | tf_op jit(solution)/shard_map/all_to_all | solution.py:310
  58.3 0.2 reduce_sum.18
  58.6 1.2 broadcast_in_dim.20
  59.7 0.0 copy-start.3
  59.7 4.8 %all-to-all-start.2 = ((f32[64,4,1152]{2,1,0:T(4,128)}), f32[64,4,1152]{2,1,0:T(4,128)S(1)}, u32[]{:S(2)}, u32[]{:S(2)}) async-start(f32[64,4,1152]{2,1,0:T(4,128)} %broadcast_in_dim.20), calls=%async_computation.2 | async-start | bytes 2359296 | tf_op jit(solution)/shard_map/all_to_all | solution.py:310
  64.5 0.0 copy-done.3
  64.5 2.2 %collective-permute-start.1 = (bf16[2048,128]{1,0:T(8,128)(2,1)S(1)}, bf16[2048,128]{1,0:T(8,128)(2,1)S(1)}, u32[]{:S(2)}, u32[]{:S(2)}) collective-permute-start(bf16[2048,128]{1,0:T(8,128)(2,1)S(1)} %copy-done.3), channel_id=1, source_target_pairs={{0,3},{1,0},{2,1},{3,2},{4,7},{5,4},{6,5},{7,6},{8,11},{9,8},{10,9... | collective-permute-start | bytes 1572872 | tf_op jit(solution)/shard_map/ppermute | solution.py:319
  66.7 0.0 collective-permute-start
  66.7 21.5 %collective-permute-done.1.right = bf16[2048,128]{1,0:T(8,128)(2,1)S(1)} collective-permute-done((bf16[2048,128]{1,0:T(8,128)(2,1)S(1)}, bf16[2048,128]{1,0:T(8,128)(2,1)S(1)}, u32[]{:S(2)}, u32[]{:S(2)}) %collective-permute-start.1) | collective-permute-done | bytes 524320 | tf_op jit(solution)/shard_map/ppermute | solution.py:319
  88.2 0.0 copy-start.5
  88.2 2.6 %collective-permute-start.3 = (bf16[1024,128]{1,0:T(8,128)(2,1)S(1)}, bf16[1024,128]{1,0:T(8,128)(2,1)S(1)}, u32[]{:S(2)}, u32[]{:S(2)}) collective-permute-start(bf16[1024,128]{1,0:T(8,128)(2,1)S(1)} %slice.9), channel_id=1, source_target_pairs={{0,3},{1,0},{2,1},{3,2},{4,7},{5,4},{6,5},{7,6},{8,11},{9,8},{10,9... | collective-permute-start | bytes 786440 | tf_op jit(solution)/shard_map/ppermute | solution.py:322
  90.8 0.0 collective-permute-done.left
  90.8 0.0 copy-start.6
  90.9 0.1 collective-permute-start.2
  90.9 0.7 and_select_fusion.order
  91.6 3.2 %collective-permute-done.3 = bf16[1024,128]{1,0:T(8,128)(2,1)S(1)} collective-permute-done((bf16[1024,128]{1,0:T(8,128)(2,1)S(1)}, bf16[1024,128]{1,0:T(8,128)(2,1)S(1)}, u32[]{:S(2)}, u32[]{:S(2)}) %collective-permute-start.3) | collective-permute-done | bytes 262176 | tf_op jit(solution)/shard_map/ppermute | solution.py:322
  94.8 3.2 %collective-permute-done.2 = bf16[1024,128]{1,0:T(8,128)(2,1)S(1)} collective-permute-done((bf16[1024,128]{1,0:T(8,128)(2,1)S(1)}, bf16[1024,128]{1,0:T(8,128)(2,1)S(1)}, u32[]{:S(2)}, u32[]{:S(2)}) %collective-permute-start.2) | collective-permute-done | bytes 262176 | tf_op jit(solution)/shard_map/ppermute | solution.py:321
  98.0 0.8 pad_maximum_fusion.far
  98.9 0.0 copy-done.5
  98.9 0.0 copy-done.6
  98.9 15.7 %features.1 = (bf16[2048,1024]{1,0:T(8,128)(2,1)}, bf16[2048,1024]{1,0:T(8,128)(2,1)}, f32[1024,256]{1,0:T(8,128)}) custom-call(s32[4]{0:T(128)} %and_select_fusion.order, bf16[2048,128]{1,0:T(8,128)(2,1)} %own, bf16[2048,128]{1,0:T(8,128)(2,1)} %copy-done.6, bf16[2048,128]{1,0:T(8,128)(2,1)} %copy-done.5, bf16[2048,128]{1,0:T(8,128)(2,1)} %pad_maximum_fusion.far, ...), custom_call_target="tpu_custom_call" | custom-call | tf_op jit(solution)/shard_map/features/pallas_call | solution.py:260
  114.6 0.0 all-to-all-done.2
  114.6 6.2 %all-to-all-start.3 = ((f32[16,64,256]{2,1,0:T(8,128)}), f32[16,64,256]{2,1,0:T(8,128)S(1)}, u32[]{:S(2)}, u32[]{:S(2)}) async-start(f32[16,64,256]{2,1,0:T(8,128)} %bitcast.20), calls=%async_computation.3 | async-start | bytes 2097152 | tf_op jit(solution)/shard_map/all_to_all | solution.py:310
  120.7 0.4 reshape.31.refs_1_
  121.2 0.0 copy-start.1
  121.2 3.4 %collective-permute-start.5 = (f32[2,128,1152]{2,1,0:T(8,128)S(1)}, f32[2,128,1152]{2,1,0:T(8,128)}, u32[]{:S(2)}, u32[]{:S(2)}) collective-permute-start(f32[2,128,1152]{2,1,0:T(8,128)S(1)} %reshape.31.refs_1_), channel_id=1, source_target_pairs={{0,4},{4,0},{1,5},{5,1},{2,6},{6,2},{3,7},{7,3},{8,12},{12,8},{9,1... | collective-permute-start | bytes 3538952 | tf_op jit(solution)/shard_map/ppermute | solution.py:336
  124.6 10.1 %all-to-all-done.3 = f32[16,64,256]{2,1,0:T(8,128)S(1)} async-done(((f32[16,64,256]{2,1,0:T(8,128)}), f32[16,64,256]{2,1,0:T(8,128)S(1)}, u32[]{:S(2)}, u32[]{:S(2)}) %all-to-all-start.3) | async-done | bytes 1048608 | tf_op jit(solution)/shard_map/all_to_all | solution.py:310
  134.6 0.1 reduce_sum.19
  134.7 4.6 %collective-permute-start.6 = (f32[64,256]{1,0:T(8,128)S(1)}, f32[64,256]{1,0:T(8,128)S(1)}, u32[]{:S(2)}, u32[]{:S(2)}) collective-permute-start(f32[64,256]{1,0:T(8,128)S(1)} %reduce_sum.19), channel_id=1, source_target_pairs={{0,4},{4,0},{1,5},{5,1},{2,6},{6,2},{3,7},{7,3},{8,12},{12,8},{9,1... | collective-permute-start | bytes 196616 | tf_op jit(solution)/shard_map/ppermute | solution.py:343
  139.3 0.9 collective-permute-done.6
  140.2 1.1 broadcast_in_dim.21
  141.3 0.0 copy-done.1
  141.3 3.7 %all-to-all-start.4 = ((f32[16,64,256]{2,1,0:T(8,128)}), f32[16,64,256]{2,1,0:T(8,128)S(1)}, u32[]{:S(2)}, u32[]{:S(2)}) async-start(f32[16,64,256]{2,1,0:T(8,128)} %broadcast_in_dim.21), calls=%async_computation.4 | async-start | bytes 2097152 | tf_op jit(solution)/shard_map/all_to_all | solution.py:310
  144.9 0.0 collective-permute-done.5.refs_2_
  144.9 49.5 %factor.1 = (f32[8,128,1024]{2,1,0:T(8,128)}, f32[8,128,128]{2,1,0:T(8,128)}) custom-call(s32[1]{0:T(128)} %bitcast.7.refs_0_, f32[2,128,1152]{2,1,0:T(8,128)} %copy-done.1, f32[2,128,1152]{2,1,0:T(8,128)} %collective-permute-done.5.refs_2_), custom_call_target="tpu_custom_call" | custom-call | tf_op jit(solution)/shard_map/factor/pallas_call | solution.py:217
  194.5 0.0 all-to-all-done.4
  194.5 0.0 copy-start.2
  194.5 1.0 copy-done.2
  195.4 11.8 %solve.1.coef = f32[1024,256]{1,0:T(8,128)} custom-call(f32[8,128,1024]{2,1,0:T(8,128)} %get-tuple-element.13.panel, f32[8,128,128]{2,1,0:T(8,128)} %get-tuple-element.14.inverse, f32[1024,256]{1,0:T(8,128)} %bitcast.18), custom_call_target="tpu_custom_call" | custom-call | tf_op jit(solution)/shard_map/solve/pallas_call | solution.py:234
  207.2 10.0 %update.1 = f32[2048,256]{1,0:T(8,128)} custom-call(bf16[2048,1024]{1,0:T(8,128)(2,1)} %get-tuple-element.10.high, bf16[2048,1024]{1,0:T(8,128)(2,1)} %get-tuple-element.11.low, f32[1024,256]{1,0:T(8,128)} %solve.1.coef, f32[2048,256]{1,0:T(8,128)} %residual.3), custom_call_target="tpu_custom_call" | custom-call | tf_op jit(solution)/shard_map/update/pallas_call | solution.py:288
  (3 shorter events, 0.0 us)
Async XLA Ops:
  0.6 13.2 %all-to-all-start = ((bf16[4,512,128]{2,1,0:T(8,128)(2,1)}), bf16[4,512,128]{2,1,0:T(8,128)(2,1)S(1)}, u32[]{:S(2)}, u32[]{:S(2)}) async-start(bf16[4,512,128]{2,1,0:T(8,128)(2,1)} %bitcast.19), calls=%async_computation | async-start | bytes 1048576 | tf_op jit(solution)/shard_map/all_to_all | solution.py:310
  13.8 0.8 copy-start.4
  21.6 6.3 %copy-start = (f32[4,128,1152]{2,1,0:T(8,128)S(1)}, f32[4,128,1152]{2,1,0:T(8,128)}, u32[]{:S(2)}) copy-start(f32[4,128,1152]{2,1,0:T(8,128)} %gram.1) | copy-start | bytes 7077892
  23.1 4.8 %collective-permute-start.4 = (f32[2,128,1152]{2,1,0:T(8,128)S(1)}, f32[2,128,1152]{2,1,0:T(8,128)}, u32[]{:S(2)}, u32[]{:S(2)}) collective-permute-start(f32[2,128,1152]{2,1,0:T(8,128)S(1)} %dynamic-slice_bitcast_fusion), channel_id=1, source_target_pairs={{0,4},{4,0},{1,5},{5,1},{2,6},{6,2},{3,7},{7,3},{8,12},{12,8},{9,1... | collective-permute-start | bytes 3538952 | tf_op jit(solution)/shard_map/ppermute | solution.py:330
  59.7 4.8 %copy-start.3 = (bf16[2048,128]{1,0:T(8,128)(2,1)S(1)}, bf16[2048,128]{1,0:T(8,128)(2,1)}, u32[]{:S(2)}) copy-start(bf16[2048,128]{1,0:T(8,128)(2,1)} %own) | copy-start | bytes 1572868
  59.7 54.8 %all-to-all-start.2 = ((f32[64,4,1152]{2,1,0:T(4,128)}), f32[64,4,1152]{2,1,0:T(4,128)S(1)}, u32[]{:S(2)}, u32[]{:S(2)}) async-start(f32[64,4,1152]{2,1,0:T(4,128)} %broadcast_in_dim.20), calls=%async_computation.2 | async-start | bytes 2359296 | tf_op jit(solution)/shard_map/all_to_all | solution.py:310
  64.5 23.7 %collective-permute-start.1 = (bf16[2048,128]{1,0:T(8,128)(2,1)S(1)}, bf16[2048,128]{1,0:T(8,128)(2,1)S(1)}, u32[]{:S(2)}, u32[]{:S(2)}) collective-permute-start(bf16[2048,128]{1,0:T(8,128)(2,1)S(1)} %copy-done.3), channel_id=1, source_target_pairs={{0,3},{1,0},{2,1},{3,2},{4,7},{5,4},{6,5},{7,6},{8,11},{9,8},{10,9... | collective-permute-start | bytes 1572872 | tf_op jit(solution)/shard_map/ppermute | solution.py:319
  66.7 24.1 %collective-permute-start = (bf16[2048,128]{1,0:T(8,128)(2,1)S(1)}, bf16[2048,128]{1,0:T(8,128)(2,1)S(1)}, u32[]{:S(2)}, u32[]{:S(2)}) collective-permute-start(bf16[2048,128]{1,0:T(8,128)(2,1)S(1)} %copy-done.3), channel_id=1, source_target_pairs={{0,1},{1,2},{2,3},{3,0},{4,5},{5,6},{6,7},{7,4},{8,9},{9,10},{10,1... | collective-permute-start | bytes 1572872 | tf_op jit(solution)/shard_map/ppermute | solution.py:318
  88.2 10.7 %copy-start.5 = (bf16[2048,128]{1,0:T(8,128)(2,1)}, bf16[2048,128]{1,0:T(8,128)(2,1)S(1)}, u32[]{:S(2)}) copy-start(bf16[2048,128]{1,0:T(8,128)(2,1)S(1)} %collective-permute-done.1.right) | copy-start | bytes 1572868
  88.2 6.6 %collective-permute-start.3 = (bf16[1024,128]{1,0:T(8,128)(2,1)S(1)}, bf16[1024,128]{1,0:T(8,128)(2,1)S(1)}, u32[]{:S(2)}, u32[]{:S(2)}) collective-permute-start(bf16[1024,128]{1,0:T(8,128)(2,1)S(1)} %slice.9), channel_id=1, source_target_pairs={{0,3},{1,0},{2,1},{3,2},{4,7},{5,4},{6,5},{7,6},{8,11},{9,8},{10,9... | collective-permute-start | bytes 786440 | tf_op jit(solution)/shard_map/ppermute | solution.py:322
  90.8 8.1 %copy-start.6 = (bf16[2048,128]{1,0:T(8,128)(2,1)}, bf16[2048,128]{1,0:T(8,128)(2,1)S(1)}, u32[]{:S(2)}) copy-start(bf16[2048,128]{1,0:T(8,128)(2,1)S(1)} %collective-permute-done.left) | copy-start | bytes 1572868
  90.9 7.2 %collective-permute-start.2 = (bf16[1024,128]{1,0:T(8,128)(2,1)S(1)}, bf16[1024,128]{1,0:T(8,128)(2,1)S(1)}, u32[]{:S(2)}, u32[]{:S(2)}) collective-permute-start(bf16[1024,128]{1,0:T(8,128)(2,1)S(1)} %slice.8), channel_id=1, source_target_pairs={{0,1},{1,2},{2,3},{3,0},{4,5},{5,6},{6,7},{7,4},{8,9},{9,10},{10,1... | collective-permute-start | bytes 786440 | tf_op jit(solution)/shard_map/ppermute | solution.py:321
  114.6 20.1 %all-to-all-start.3 = ((f32[16,64,256]{2,1,0:T(8,128)}), f32[16,64,256]{2,1,0:T(8,128)S(1)}, u32[]{:S(2)}, u32[]{:S(2)}) async-start(f32[16,64,256]{2,1,0:T(8,128)} %bitcast.20), calls=%async_computation.3 | async-start | bytes 2097152 | tf_op jit(solution)/shard_map/all_to_all | solution.py:310
  121.2 20.1 %copy-start.1 = (f32[2,128,1152]{2,1,0:T(8,128)}, f32[2,128,1152]{2,1,0:T(8,128)S(1)}, u32[]{:S(2)}) copy-start(f32[2,128,1152]{2,1,0:T(8,128)S(1)} %reshape.31.refs_1_) | copy-start | bytes 3538948
  121.2 23.8 %collective-permute-start.5 = (f32[2,128,1152]{2,1,0:T(8,128)S(1)}, f32[2,128,1152]{2,1,0:T(8,128)}, u32[]{:S(2)}, u32[]{:S(2)}) collective-permute-start(f32[2,128,1152]{2,1,0:T(8,128)S(1)} %reshape.31.refs_1_), channel_id=1, source_target_pairs={{0,4},{4,0},{1,5},{5,1},{2,6},{6,2},{3,7},{7,3},{8,12},{12,8},{9,1... | collective-permute-start | bytes 3538952 | tf_op jit(solution)/shard_map/ppermute | solution.py:336
  134.7 5.5 %collective-permute-start.6 = (f32[64,256]{1,0:T(8,128)S(1)}, f32[64,256]{1,0:T(8,128)S(1)}, u32[]{:S(2)}, u32[]{:S(2)}) collective-permute-start(f32[64,256]{1,0:T(8,128)S(1)} %reduce_sum.19), channel_id=1, source_target_pairs={{0,4},{4,0},{1,5},{5,1},{2,6},{6,2},{3,7},{7,3},{8,12},{12,8},{9,1... | collective-permute-start | bytes 196616 | tf_op jit(solution)/shard_map/ppermute | solution.py:343
  141.3 53.2 %all-to-all-start.4 = ((f32[16,64,256]{2,1,0:T(8,128)}), f32[16,64,256]{2,1,0:T(8,128)S(1)}, u32[]{:S(2)}, u32[]{:S(2)}) async-start(f32[16,64,256]{2,1,0:T(8,128)} %broadcast_in_dim.21), calls=%async_computation.4 | async-start | bytes 2097152 | tf_op jit(solution)/shard_map/all_to_all | solution.py:310
  194.5 1.0 copy-start.2

commit v3 on v2

--- a/solution.py
+++ b/solution.py
@@ -6,6 +6,7 @@
 from jax.experimental import pallas as pl
 from jax.experimental.pallas import tpu as pltpu
 from jax.sharding import PartitionSpec as P
+
 
 F32 = jnp.float32
 BF16 = jnp.bfloat16
@@ -127,28 +128,11 @@
         d[k0 : k0 + PB, :] = x
 
 
-def factor_kernel(core, mine, other, panel, inverse, a, d, *, ridge):
-    blocks = panel.shape[0]
-    size = blocks * NB
-    quarter = blocks // 4
-
-    def unpack(halves):
-        for i in range(blocks):
-            at, col = packed_slot(i, blocks)
-            a[i, :, i * NB : size] = halves[at // quarter][at % quarter, :, col : col + size - i * NB]
-
-    @pl.when(core[0] == 0)
-    def _():
-        unpack((mine, other))
-
-    @pl.when(core[0] != 0)
-    def _():
-        unpack((other, mine))
-
-    for i in range(blocks):
-        if i > 0:
-            a[i, :, : i * NB] = jnp.zeros((NB, i * NB), F32)
-            panel[i, :, : i * NB] = jnp.zeros((NB, i * NB), F32)
+def factor_steps(panel, inverse, a, d, ridge):
+    steps = panel.shape[0]
+    blocks = a.shape[0]
+    for i in range(1, blocks):
+        a[i, :, : i * NB] = jnp.zeros((NB, i * NB), F32)
     eye = jnp.where(
         lax.broadcasted_iota(jnp.int32, (NB, NB), 0) == lax.broadcasted_iota(jnp.int32, (NB, NB), 1),
         ridge,
@@ -163,6 +147,8 @@
 
         def eliminate(first):
             panel[i, :, first:] = dot(d[...], a[i, :, first:], HIGHEST)
+            if first > 0:
+                panel[i, :, :first] = jnp.zeros((NB, first), F32)
 
             def row(j, _):
                 left = a[i, :, pl.ds(pl.multiple_of(j * NB, NB), NB)]
@@ -171,33 +157,67 @@
 
             lax.fori_loop(i + 1, blocks, row, 0)
 
-        for part in range(4):
-            low = part * (blocks // 4)
-
-            @pl.when((i >= low) & (i < low + blocks // 4))
+        for low in range(0, steps, 2):
+
+            @pl.when((i >= low) & (i < low + 2))
             def _():
                 eliminate(low * NB)
 
         return 0
 
-    lax.fori_loop(0, blocks, step, 0)
-
-
-def solve_kernel(panel, inverse, corr, out, c):
-    blocks = panel.shape[0]
-    c[...] = jnp.zeros_like(c)
+    lax.fori_loop(0, steps, step, 0)
+
+
+def first_factor_kernel(core, mine, other, panel, inverse, rest, a, d, *, ridge):
+    blocks = a.shape[0]
+    size = blocks * NB
+    quarter = blocks // 4
+
+    def unpack(halves):
+        for i in range(blocks):
+            at, col = packed_slot(i, blocks)
+            a[i, :, i * NB : size] = halves[at // quarter][at % quarter, :, col : col + size - i * NB]
+
+    @pl.when(core[0] == 0)
+    def _():
+        unpack((mine, other))
+
+    @pl.when(core[0] != 0)
+    def _():
+        unpack((other, mine))
+
+    factor_steps(panel, inverse, a, d, ridge)
+    steps = panel.shape[0]
+    for i in range(steps, blocks):
+        rest[i - steps] = a[i, :, steps * NB :]
+
+
+def second_factor_kernel(matrix, panel, inverse, a, d, *, ridge):
+    a[...] = matrix[...]
+    factor_steps(panel, inverse, a, d, ridge)
+
+
+def solve_kernel(panel0, inverse0, panel1, inverse1, corr, out, c):
+    half = panel0.shape[0]
+    blocks = half + panel1.shape[0]
+
+    def panel(i, first, last):
+        if i < half:
+            return panel0[i, :, first * NB : last * NB]
+        return panel1[i - half, :, (first - half) * NB : (last - half) * NB]
+
     for i in range(blocks):
         rows = slice(i * NB, (i + 1) * NB)
         value = corr[rows, :]
         for j in range(i):
-            value = value - dot_t(panel[j, :, rows], c[j * NB : (j + 1) * NB, :], HIGHEST)
+            value = value - dot_t(panel(j, i, i + 1), c[j * NB : (j + 1) * NB, :], HIGHEST)
         c[rows, :] = value
     for i in range(blocks - 1, -1, -1):
         rows = slice(i * NB, (i + 1) * NB)
-        value = dot(inverse[i], c[rows, :], HIGHEST)
+        inverse = inverse0[i] if i < half else inverse1[i - half]
+        value = dot(inverse, c[rows, :], HIGHEST)
         if i < blocks - 1:
-            rest = (i + 1) * NB
-            value = value - dot(panel[i, :, rest:], out[rest:, :], HIGHEST)
+            value = value - dot(panel(i, i + 1, blocks), out[(i + 1) * NB :, :], HIGHEST)
         out[rows, :] = value
 
 
@@ -207,37 +227,64 @@
     out[...] = residual[...] - (dot(h, wh) + dot(h, wl) + dot(low[...], wh))
 
 
+def cost(us):
+    return pl.CostEstimate(flops=int(us * 5e8), bytes_accessed=0, transcendentals=0)
+
+
 def params(**kw):
     return pltpu.CompilerParams(vmem_limit_bytes=56 * 1024 * 1024, **kw)
 
 
-def factor_call(core, mine, other, ridge):
+def factor_shapes(steps, blocks):
+    return (
+        jax.ShapeDtypeStruct((steps, NB, blocks * NB), F32),
+        jax.ShapeDtypeStruct((steps, NB, NB), F32),
+    )
+
+
+def factor_scratch(blocks):
+    return [pltpu.VMEM((blocks, NB, blocks * NB), F32), pltpu.VMEM((NB, NB), F32)]
+
+
+def first_factor_call(core, mine, other, ridge):
     blocks = mine.shape[0] * 4
+    steps = blocks // 2
     vmem = pl.BlockSpec(memory_space=pltpu.VMEM)
     return pl.pallas_call(
-        lambda *refs: factor_kernel(*refs, ridge=ridge),
+        lambda *refs: first_factor_kernel(*refs, ridge=ridge),
         in_specs=[pl.BlockSpec(memory_space=pltpu.SMEM), vmem, vmem],
         out_shape=(
-            jax.ShapeDtypeStruct((blocks, NB, blocks * NB), F32),
-            jax.ShapeDtypeStruct((blocks, NB, NB), F32),
+            *factor_shapes(steps, blocks),
+            jax.ShapeDtypeStruct((blocks - steps, NB, (blocks - steps) * NB), F32),
         ),
-        scratch_shapes=[
-            pltpu.VMEM((blocks, NB, blocks * NB), F32),
-            pltpu.VMEM((NB, NB), F32),
-        ],
+        scratch_shapes=factor_scratch(blocks),
         compiler_params=params(),
-        name="factor",
+        cost_estimate=cost(28),
+        name="factor0",
     )(core, mine, other)
 
 
-def solve_call(panel, inverse, corr):
+def second_factor_call(matrix, ridge):
+    blocks = matrix.shape[0]
+    return pl.pallas_call(
+        lambda *refs: second_factor_kernel(*refs, ridge=ridge),
+        out_shape=factor_shapes(blocks, blocks),
+        scratch_shapes=factor_scratch(blocks),
+        compiler_params=params(),
+        cost_estimate=cost(22),
+        name="factor1",
+    )(matrix)
+
+
+def solve_call(factors, corr):
     return pl.pallas_call(
         solve_kernel,
         out_shape=jax.ShapeDtypeStruct(corr.shape, F32),
         scratch_shapes=[pltpu.VMEM(corr.shape, F32)],
         compiler_params=params(),
+        cost_estimate=cost(12),
         name="solve",
-    )(panel, inverse, corr)
+    )(*factors, corr)
 
 
 def gram_call(frames, weights, phases):
@@ -249,6 +296,7 @@
         out_shape=jax.ShapeDtypeStruct((blocks // 2, NB, feat + NB), F32),
         scratch_shapes=[pltpu.VMEM((rows, feat), BF16), pltpu.VMEM((rows, feat), BF16)],
         compiler_params=params(),
+        cost_estimate=cost(7),
         name="gram",
     )(frames, weights, phases)
 
@@ -278,6 +326,7 @@
             jax.ShapeDtypeStruct((feat, cols), F32),
         ],
         compiler_params=params(dimension_semantics=("arbitrary",)),
+        cost_estimate=cost(15),
         name="features",
     )(order, *slabs, weights.reshape(4, width, feat), phases, residual)
 
@@ -297,6 +346,7 @@
         out_specs=pl.BlockSpec((tile, cols), lambda i: (i, 0)),
         out_shape=jax.ShapeDtypeStruct((rows, cols), F32),
         compiler_params=params(dimension_semantics=("arbitrary",)),
+        cost_estimate=cost(10),
         name="update",
     )(high, low, coef, residual)
 
@@ -331,7 +381,8 @@
     chips = ("y", "z", "tgt")
     count = lax.axis_size(chips)
     parts = mine.reshape(count, -1, mine.shape[-1])
-    piece = jnp.sum(exchange(parts, chips), axis=0)
+    parts = exchange(parts, chips)
+    piece = jnp.sum(parts, axis=0)
     mine = to_everyone(piece, chips).reshape(mine.shape)
     return mine, lax.ppermute(mine, "core", SWAP)
 
@@ -339,12 +390,13 @@
 def summed_corr(corr):
     plane = ("y", "z")
     count = lax.axis_size(plane)
-    piece = jnp.sum(exchange(corr.reshape(count, -1, corr.shape[-1]), plane), axis=0)
+    parts = exchange(corr.reshape(count, -1, corr.shape[-1]), plane)
+    piece = jnp.sum(parts, axis=0)
     piece = piece + lax.ppermute(piece, "core", SWAP)
     return to_everyone(piece, plane).reshape(corr.shape)
 
 
-def body(frames, weights, phases, residual):
+def block_step(frames, weights, phases, residual):
     rows_here = frames.shape[0]
     feature_count = weights.shape[1]
     ridge = 0.1 * rows_here * lax.axis_size(("y", "z", "core")) / feature_count
@@ -359,8 +411,9 @@
     order = jnp.stack([at, at + 3, at + 1, at + 2]) % 4
     high, low, corr = feature_call(order, slabs, weights, phases, residual)
     corr = summed_corr(corr)
-    panel, inverse = factor_call(core[None], mine, other, ridge)
-    coefficients = solve_call(panel, inverse, corr)
+    panel0, inverse0, rest = first_factor_call(core[None], mine, other, ridge)
+    panel1, inverse1 = second_factor_call(rest, ridge)
+    coefficients = solve_call((panel0, inverse0, panel1, inverse1), corr)
     residual_next = update_call(high, low, coefficients, residual)
     return (residual_next, coefficients)
 
@@ -369,7 +422,7 @@
     rows = ("y", "z", "core")
     mesh = jax.sharding.Mesh(mesh.devices.reshape(4, 4, 2, 4), (*rows, "tgt"))
     return jax.shard_map(
-        body,
+        block_step,
         mesh=mesh,
         in_specs=(P(rows, "tgt"), P(), P(), P(rows, "tgt")),
         out_specs=(P(rows, "tgt"), P(None, "tgt")),

time: 218 us -> 224 us (1.028)
  blocking collectives: 28.7 us -> 51.1 us
  waiting for transfers between devices: 49.8 us -> 39.6 us
  starting transfers between devices: 34.5 us -> 25.5 us
    all_to_all x1 -> x2, blocking collectives: 28.7 us -> 51.1 us  [exchange(): return lax.all_to_all(parts, axes, 0, 0, tiled=True)]
    all_to_all x4 -> x3, waiting for transfers between devices: 18.4 us -> 8.33 us  [exchange(): return lax.all_to_all(parts, axes, 0, 0, tiled=True)]
    all_to_all x4 -> x3, starting transfers between devices: 19.5 us -> 13.3 us  [exchange(): return lax.all_to_all(parts, axes, 0, 0, tiled=True)]
    ppermute x1, starting transfers between devices: 4.59 us -> 2.32 us  [summed_corr(): piece = piece + lax.ppermute(piece, 'core', SWAP)]
    pallas_call x1 -> x2, Pallas kernels: 49.5 us -> 51.4 us  [the longest x1 31.9 us: first_factor_call(): pl.pallas_call(lambda *refs: first_factor_kernel(*refs, ridge=ridge), in_...]
  transfers between devices with their start and end apart: 11 -> 10, of which waited for: 7 -> 6; matrix products, arithmetic and copies ran while one was open for 1% -> 1% of each run, Pallas kernels for 30% -> 30%
where the time goes in v3:
time: 224 us; the launch traced here: 223 us
  Pallas kernels  95.5 us (43%)
  blocking collectives  51.1 us (23%)
  waiting for transfers between devices  39.6 us (18%)
  starting transfers between devices  25.5 us (11%)
  local copies, waits for them, and re-layouts  6.98 us (3%)
  other arithmetic  3.17 us (1%)
    all_to_all x2, blocking collectives, exchange(): return lax.all_to_all(parts, axes, 0, 0, tiled=True)  51.1 us
    pallas_call x1, Pallas kernels, first_factor_call(): pl.pallas_call(lambda *refs: first_factor_kernel(*refs, ridge=ridge), in_...  31.9 us
    ppermute x1, waiting for transfers between devices, ring_slabs(): right = lax.ppermute(own, 'tgt', DOWN)  21.5 us
    pallas_call x1, Pallas kernels, second_factor_call(): pl.pallas_call(lambda *refs: second_factor_kernel(*refs, ridge=ridge), ou...  19.4 us
    pallas_call x1, Pallas kernels, feature_call(): pl.pallas_call(feature_kernel, grid=(rows // tile,), in_specs=[pl.BlockSp...  15.7 us
    all_to_all x3, starting transfers between devices, exchange(): return lax.all_to_all(parts, axes, 0, 0, tiled=True)  13.3 us
    pallas_call x1, Pallas kernels, solve_call(): pl.pallas_call(solve_kernel, out_shape=jax.ShapeDtypeStruct(corr.shape, F...  11.5 us
    pallas_call x1, Pallas kernels, update_call(): pl.pallas_call(update_kernel, grid=(rows // tile,), in_specs=[pl.BlockSpe...  9.99 us
  transfers between devices with their start and end apart: 10, of which 6 were waited for; matrix products, arithmetic and copies ran while one was open for 1% of the time, Pallas kernels for 30%

profile of v3, /device:TPU:1, one launch (start us, length us, event | category | flops | bytes accessed | tf_op | source)
XLA Modules:
  0.0 222.7 jit_solution(18029268309646803090)
XLA Ops:
  0.6 4.8 %all-to-all-start = ((bf16[4,512,128]{2,1,0:T(8,128)(2,1)}), bf16[4,512,128]{2,1,0:T(8,128)(2,1)S(1)}, u32[]{:S(2)}, u32[]{:S(2)}) async-start(bf16[4,512,128]{2,1,0:T(8,128)(2,1)} %bitcast.19), calls=%async_computation | async-start | bytes 1048576 | tf_op jit(solution)/shard_map/all_to_all | solution.py:360
  5.5 8.3 %all-to-all-done.frames = bf16[4,512,128]{2,1,0:T(8,128)(2,1)S(1)} async-done(((bf16[4,512,128]{2,1,0:T(8,128)(2,1)}), bf16[4,512,128]{2,1,0:T(8,128)(2,1)S(1)}, u32[]{:S(2)}, u32[]{:S(2)}) %all-to-all-start) | async-done | bytes 524320 | tf_op jit(solution)/shard_map/all_to_all | solution.py:360
  13.8 0.0 copy-start.3
  13.8 0.8 copy-done.3
  14.6 7.0 %gram.1 = f32[4,128,1152]{2,1,0:T(8,128)} custom-call(bf16[4,512,128]{2,1,0:T(8,128)(2,1)} %copy-done.3, bf16[512,1024]{1,0:T(8,128)(2,1)} %weights.1, f32[1,1024]{1,0:T(1,128)} %bitcast.21), custom_call_target="tpu_custom_call" | custom-call | flops 3500000000 | tf_op jit(solution)/shard_map/gram/pallas_call | solution.py:294
  21.6 1.3 dynamic-slice_bitcast_fusion
  23.0 2.2 collective-permute-start.4
  25.2 2.5 %collective-permute-done.4 = f32[2,128,1152]{2,1,0:T(8,128)S(1)} collective-permute-done((f32[2,128,1152]{2,1,0:T(8,128)S(1)}, f32[2,128,1152]{2,1,0:T(8,128)S(1)}, u32[]{:S(2)}, u32[]{:S(2)}) %collective-permute-start.4) | collective-permute-done | bytes 1179680 | tf_op jit(solution)/shard_map/ppermute | solution.py:380
  27.6 1.4 bitcast_add_fusion
  29.0 0.3 reshape.30
  29.4 28.7 %all_to_all.25 = f32[64,4,1152]{2,1,0:T(4,128)S(1)} all-to-all(f32[64,4,1152]{2,1,0:T(4,128)S(1)} %reshape.30), channel_id=1, replica_groups=mesh['y'=4,'z'=4,'core'=2,'tgt'=4] {'y','z','tgt'}, dimensions={0} | all-to-all | bytes 2359296 | tf_op jit(solution)/shard_map/all_to_all | solution.py:360
  58.1 0.2 reduce_sum.18
  58.3 1.2 broadcast_in_dim.20
  59.4 0.0 copy-start.2
  59.4 4.8 %all-to-all-start.2 = ((f32[64,4,1152]{2,1,0:T(4,128)}), f32[64,4,1152]{2,1,0:T(4,128)S(1)}, u32[]{:S(2)}, u32[]{:S(2)}) async-start(f32[64,4,1152]{2,1,0:T(4,128)} %broadcast_in_dim.20), calls=%async_computation.2 | async-start | bytes 2359296 | tf_op jit(solution)/shard_map/all_to_all | solution.py:360
  64.2 0.0 copy-done.2
  64.2 2.2 collective-permute-start.1
  66.4 0.0 collective-permute-start
  66.4 21.5 %collective-permute-done.1.right = bf16[2048,128]{1,0:T(8,128)(2,1)S(1)} collective-permute-done((bf16[2048,128]{1,0:T(8,128)(2,1)S(1)}, bf16[2048,128]{1,0:T(8,128)(2,1)S(1)}, u32[]{:S(2)}, u32[]{:S(2)}) %collective-permute-start.1) | collective-permute-done | bytes 524320 | tf_op jit(solution)/shard_map/ppermute | solution.py:369
  87.9 0.0 copy-start.4
  88.0 2.6 %collective-permute-start.3 = (bf16[1024,128]{1,0:T(8,128)(2,1)S(1)}, bf16[1024,128]{1,0:T(8,128)(2,1)S(1)}, u32[]{:S(2)}, u32[]{:S(2)}) collective-permute-start(bf16[1024,128]{1,0:T(8,128)(2,1)S(1)} %slice.9), channel_id=1, source_target_pairs={{0,3},{1,0},{2,1},{3,2},{4,7},{5,4},{6,5},{7,6},{8,11},{9,8},{10,9... | collective-permute-start | bytes 786440 | tf_op jit(solution)/shard_map/ppermute | solution.py:372
  90.6 0.0 collective-permute-done.left
  90.6 0.0 copy-start.5
  90.6 0.8 copy-done.5
  91.4 0.1 collective-permute-start.2
  91.5 0.7 and_select_fusion.order
  92.1 2.4 %collective-permute-done.3 = bf16[1024,128]{1,0:T(8,128)(2,1)S(1)} collective-permute-done((bf16[1024,128]{1,0:T(8,128)(2,1)S(1)}, bf16[1024,128]{1,0:T(8,128)(2,1)S(1)}, u32[]{:S(2)}, u32[]{:S(2)}) %collective-permute-start.3) | collective-permute-done | bytes 262176 | tf_op jit(solution)/shard_map/ppermute | solution.py:372
  94.5 4.0 %collective-permute-done.2 = bf16[1024,128]{1,0:T(8,128)(2,1)S(1)} collective-permute-done((bf16[1024,128]{1,0:T(8,128)(2,1)S(1)}, bf16[1024,128]{1,0:T(8,128)(2,1)S(1)}, u32[]{:S(2)}, u32[]{:S(2)}) %collective-permute-start.2) | collective-permute-done | bytes 262176 | tf_op jit(solution)/shard_map/ppermute | solution.py:371
  98.6 0.8 pad_maximum_fusion.far
  99.4 0.0 all-to-all-done.2
  99.4 0.4 reshape.31.refs_1_
  99.8 0.0 copy-done.4
  99.8 0.0 copy-start
  99.8 2.9 %collective-permute-start.5 = (f32[2,128,1152]{2,1,0:T(8,128)S(1)}, f32[2,128,1152]{2,1,0:T(8,128)}, u32[]{:S(2)}, u32[]{:S(2)}) collective-permute-start(f32[2,128,1152]{2,1,0:T(8,128)S(1)} %reshape.31.refs_1_), channel_id=1, source_target_pairs={{0,4},{4,0},{1,5},{5,1},{2,6},{6,2},{3,7},{7,3},{8,12},{12,8},{9,1... | collective-permute-start | bytes 3538952 | tf_op jit(solution)/shard_map/ppermute | solution.py:387
  102.7 15.7 %features.1 = (bf16[2048,1024]{1,0:T(8,128)(2,1)}, bf16[2048,1024]{1,0:T(8,128)(2,1)}, f32[1024,256]{1,0:T(8,128)}) custom-call(s32[4]{0:T(128)} %and_select_fusion.order, bf16[2048,128]{1,0:T(8,128)(2,1)} %own, bf16[2048,128]{1,0:T(8,128)(2,1)} %copy-done.5, bf16[2048,128]{1,0:T(8,128)(2,1)} %copy-done.4, bf16[2048,128]{1,0:T(8,128)(2,1)} %pad_maximum_fusion.far, ...), custom_call_target="tpu_custom_call" | custom-call | flops 7500000256 | tf_op jit(solution)/shard_map/features/pallas_call | solution.py:308
  118.4 0.0 copy-done
  118.4 22.4 %all_to_all.26 = f32[16,64,256]{2,1,0:T(8,128)S(1)} all-to-all(f32[16,64,256]{2,1,0:T(8,128)} %bitcast.18), channel_id=1, replica_groups=mesh['y'=4,'z'=4,'core'=2,'tgt'=4] {'y','z'}, dimensions={0} | all-to-all | bytes 2097152 | tf_op jit(solution)/shard_map/all_to_all | solution.py:360
  140.8 0.1 reduce_sum.19
  140.9 2.3 %collective-permute-start.6 = (f32[64,256]{1,0:T(8,128)S(1)}, f32[64,256]{1,0:T(8,128)S(1)}, u32[]{:S(2)}, u32[]{:S(2)}) collective-permute-start(f32[64,256]{1,0:T(8,128)S(1)} %reduce_sum.19), channel_id=1, source_target_pairs={{0,4},{4,0},{1,5},{5,1},{2,6},{6,2},{3,7},{7,3},{8,12},{12,8},{9,1... | collective-permute-start | bytes 196616 | tf_op jit(solution)/shard_map/ppermute | solution.py:395
  143.2 0.9 collective-permute-done.6
  144.1 1.1 broadcast_in_dim.21
  145.2 3.7 %all-to-all-start.4 = ((f32[16,64,256]{2,1,0:T(8,128)}), f32[16,64,256]{2,1,0:T(8,128)S(1)}, u32[]{:S(2)}, u32[]{:S(2)}) async-start(f32[16,64,256]{2,1,0:T(8,128)} %broadcast_in_dim.21), calls=%async_computation.4 | async-start | bytes 2097152 | tf_op jit(solution)/shard_map/all_to_all | solution.py:360
  148.9 0.0 collective-permute-done.5.refs_2_
  148.9 31.9 %factor0.1 = (f32[4,128,1024]{2,1,0:T(8,128)}, f32[4,128,128]{2,1,0:T(8,128)}, f32[4,128,512]{2,1,0:T(8,128)}) custom-call(s32[1]{0:T(128)} %bitcast.7.refs_0_, f32[2,128,1152]{2,1,0:T(8,128)} %copy-done, f32[2,128,1152]{2,1,0:T(8,128)} %collective-permute-done.5.refs_2_), custom_call_target="tpu_custom_call" | custom-call | flops 14000000000 | tf_op jit(solution)/shard_map/factor0/pallas_call | solution.py:253
  180.8 19.4 %factor1.1 = (f32[4,128,512]{2,1,0:T(8,128)}, f32[4,128,128]{2,1,0:T(8,128)}) custom-call(f32[4,128,512]{2,1,0:T(8,128)} %get-tuple-element.18.refs_0_), custom_call_target="tpu_custom_call" | custom-call | flops 11000000512 | tf_op jit(solution)/shard_map/factor1/pallas_call | solution.py:269
  200.2 0.0 all-to-all-done.4
  200.2 0.0 copy-start.1
  200.2 1.0 copy-done.1
  201.2 11.5 %solve.1.coef = f32[1024,256]{1,0:T(8,128)} custom-call(f32[4,128,1024]{2,1,0:T(8,128)} %get-tuple-element.16.panel0, f32[4,128,128]{2,1,0:T(8,128)} %get-tuple-element.17.inverse0, f32[4,128,512]{2,1,0:T(8,128)} %get-tuple-element.19.panel1, f32[4,128,128]{2,1,0:T(8,128)} %get-tuple-element.20.inverse1, f32[1024,256]{1,0:T(8,128)} %bitcast.17), custom_call_target="tpu_custom_call" | custom-call | flops 6000000000 | tf_op jit(solution)/shard_map/solve/pallas_call | solution.py:280
  212.7 10.0 %update.1 = f32[2048,256]{1,0:T(8,128)} custom-call(bf16[2048,1024]{1,0:T(8,128)(2,1)} %get-tuple-element.13.high, bf16[2048,1024]{1,0:T(8,128)(2,1)} %get-tuple-element.14.low, f32[1024,256]{1,0:T(8,128)} %solve.1.coef, f32[2048,256]{1,0:T(8,128)} %residual.3), custom_call_target="tpu_custom_call" | custom-call | flops 5000000000 | tf_op jit(solution)/shard_map/update/pallas_call | solution.py:337
  (3 shorter events, 0.0 us)
Async XLA Ops:
  0.6 13.2 %all-to-all-start = ((bf16[4,512,128]{2,1,0:T(8,128)(2,1)}), bf16[4,512,128]{2,1,0:T(8,128)(2,1)S(1)}, u32[]{:S(2)}, u32[]{:S(2)}) async-start(bf16[4,512,128]{2,1,0:T(8,128)(2,1)} %bitcast.19), calls=%async_computation | async-start | bytes 1048576 | tf_op jit(solution)/shard_map/all_to_all | solution.py:360
  13.8 0.8 copy-start.3
  23.0 4.7 %collective-permute-start.4 = (f32[2,128,1152]{2,1,0:T(8,128)S(1)}, f32[2,128,1152]{2,1,0:T(8,128)S(1)}, u32[]{:S(2)}, u32[]{:S(2)}) collective-permute-start(f32[2,128,1152]{2,1,0:T(8,128)S(1)} %dynamic-slice_bitcast_fusion), channel_id=1, source_target_pairs={{0,4},{4,0},{1,5},{5,1},{2,6},{6,2},{3,7},{7,3},{8,12},{12,8},{9,1... | collective-permute-start | bytes 3538952 | tf_op jit(solution)/shard_map/ppermute | solution.py:380
  59.4 4.8 %copy-start.2 = (bf16[2048,128]{1,0:T(8,128)(2,1)S(1)}, bf16[2048,128]{1,0:T(8,128)(2,1)}, u32[]{:S(2)}) copy-start(bf16[2048,128]{1,0:T(8,128)(2,1)} %own) | copy-start | bytes 1572868
  59.4 40.0 %all-to-all-start.2 = ((f32[64,4,1152]{2,1,0:T(4,128)}), f32[64,4,1152]{2,1,0:T(4,128)S(1)}, u32[]{:S(2)}, u32[]{:S(2)}) async-start(f32[64,4,1152]{2,1,0:T(4,128)} %broadcast_in_dim.20), calls=%async_computation.2 | async-start | bytes 2359296 | tf_op jit(solution)/shard_map/all_to_all | solution.py:360
  64.2 23.7 %collective-permute-start.1 = (bf16[2048,128]{1,0:T(8,128)(2,1)S(1)}, bf16[2048,128]{1,0:T(8,128)(2,1)S(1)}, u32[]{:S(2)}, u32[]{:S(2)}) collective-permute-start(bf16[2048,128]{1,0:T(8,128)(2,1)S(1)} %copy-done.2), channel_id=1, source_target_pairs={{0,3},{1,0},{2,1},{3,2},{4,7},{5,4},{6,5},{7,6},{8,11},{9,8},{10,9... | collective-permute-start | bytes 1572872 | tf_op jit(solution)/shard_map/ppermute | solution.py:369
  66.4 24.1 %collective-permute-start = (bf16[2048,128]{1,0:T(8,128)(2,1)S(1)}, bf16[2048,128]{1,0:T(8,128)(2,1)S(1)}, u32[]{:S(2)}, u32[]{:S(2)}) collective-permute-start(bf16[2048,128]{1,0:T(8,128)(2,1)S(1)} %copy-done.2), channel_id=1, source_target_pairs={{0,1},{1,2},{2,3},{3,0},{4,5},{5,6},{6,7},{7,4},{8,9},{9,10},{10,1... | collective-permute-start | bytes 1572872 | tf_op jit(solution)/shard_map/ppermute | solution.py:368
  87.9 11.9 %copy-start.4 = (bf16[2048,128]{1,0:T(8,128)(2,1)}, bf16[2048,128]{1,0:T(8,128)(2,1)S(1)}, u32[]{:S(2)}) copy-start(bf16[2048,128]{1,0:T(8,128)(2,1)S(1)} %collective-permute-done.1.right) | copy-start | bytes 1572868
  88.0 6.6 %collective-permute-start.3 = (bf16[1024,128]{1,0:T(8,128)(2,1)S(1)}, bf16[1024,128]{1,0:T(8,128)(2,1)S(1)}, u32[]{:S(2)}, u32[]{:S(2)}) collective-permute-start(bf16[1024,128]{1,0:T(8,128)(2,1)S(1)} %slice.9), channel_id=1, source_target_pairs={{0,3},{1,0},{2,1},{3,2},{4,7},{5,4},{6,5},{7,6},{8,11},{9,8},{10,9... | collective-permute-start | bytes 786440 | tf_op jit(solution)/shard_map/ppermute | solution.py:372
  90.6 0.8 copy-start.5
  91.4 7.2 %collective-permute-start.2 = (bf16[1024,128]{1,0:T(8,128)(2,1)S(1)}, bf16[1024,128]{1,0:T(8,128)(2,1)S(1)}, u32[]{:S(2)}, u32[]{:S(2)}) collective-permute-start(bf16[1024,128]{1,0:T(8,128)(2,1)S(1)} %slice.8), channel_id=1, source_target_pairs={{0,1},{1,2},{2,3},{3,0},{4,5},{5,6},{6,7},{7,4},{8,9},{9,10},{10,1... | collective-permute-start | bytes 786440 | tf_op jit(solution)/shard_map/ppermute | solution.py:371
  99.8 18.6 %copy-start = (f32[2,128,1152]{2,1,0:T(8,128)}, f32[2,128,1152]{2,1,0:T(8,128)S(1)}, u32[]{:S(2)}) copy-start(f32[2,128,1152]{2,1,0:T(8,128)S(1)} %reshape.31.refs_1_) | copy-start | bytes 3538948
  99.8 49.0 %collective-permute-start.5 = (f32[2,128,1152]{2,1,0:T(8,128)S(1)}, f32[2,128,1152]{2,1,0:T(8,128)}, u32[]{:S(2)}, u32[]{:S(2)}) collective-permute-start(f32[2,128,1152]{2,1,0:T(8,128)S(1)} %reshape.31.refs_1_), channel_id=1, source_target_pairs={{0,4},{4,0},{1,5},{5,1},{2,6},{6,2},{3,7},{7,3},{8,12},{12,8},{9,1... | collective-permute-start | bytes 3538952 | tf_op jit(solution)/shard_map/ppermute | solution.py:387
  140.9 3.2 %collective-permute-start.6 = (f32[64,256]{1,0:T(8,128)S(1)}, f32[64,256]{1,0:T(8,128)S(1)}, u32[]{:S(2)}, u32[]{:S(2)}) collective-permute-start(f32[64,256]{1,0:T(8,128)S(1)} %reduce_sum.19), channel_id=1, source_target_pairs={{0,4},{4,0},{1,5},{5,1},{2,6},{6,2},{3,7},{7,3},{8,12},{12,8},{9,1... | collective-permute-start | bytes 196616 | tf_op jit(solution)/shard_map/ppermute | solution.py:395
  145.2 55.0 %all-to-all-start.4 = ((f32[16,64,256]{2,1,0:T(8,128)}), f32[16,64,256]{2,1,0:T(8,128)S(1)}, u32[]{:S(2)}, u32[]{:S(2)}) async-start(f32[16,64,256]{2,1,0:T(8,128)} %broadcast_in_dim.21), calls=%async_computation.4 | async-start | bytes 2097152 | tf_op jit(solution)/shard_map/all_to_all | solution.py:360
  200.2 1.0 copy-start.1
